TPU v7x, 8 devices: a whole 2x2x1 slice. The times are simulated.
8 devices in a mesh: dp: 2 (over z, y), tp: 4 (over x, core).
Axes of the slice: x: 2, y: 2, z: 1, core: 2. Of those that a mesh axis runs over, the one named last changes fastest.
Arguments:
- token_ids: int32 [8192], P('dp'), parts along dimension 0
- embed_table: bfloat16 [256000, 2048], P('tp')
- norm_gain: bfloat16 [2048], replicated
- w_in: bfloat16 [2048, 16384], P(None, 'tp')
- w_out: bfloat16 [16384, 2048], P('tp')
Outputs:
- output: bfloat16 [8192, 2048], P(('dp', 'tp')), parts along dimension 0
There are 2 independent parts. A program takes and returns all parts, laid end to end along the dimension named above; an argument that names none is the same for every part.
All inputs are finite; a program needn't handle non-finite values.
Results may differ from a plain program's by a relative error of at most 0.001.
Values are sent between devices in bfloat16 or wider.
A program may use at most 1.25 GiB of HBM per device.

v0:
```python
import jax
import jax.numpy as jnp
from jax import lax
from jax.sharding import PartitionSpec as P

RMS_EPS = 1e-6


def rms_norm(row_vals, norm_gain):
    rows_f32 = row_vals.astype(jnp.float32)
    inv_rms = lax.rsqrt(jnp.mean(rows_f32 * rows_f32, axis=-1, keepdims=True) + RMS_EPS)
    return (rows_f32 * inv_rms * norm_gain.astype(jnp.float32)).astype(jnp.bfloat16)


def solution(mesh):
    def device_step(token_ids, table_shard, norm_gain, w_in_shard, w_out_shard):
        shard_rows = table_shard.shape[0]
        row_offset = lax.axis_index("tp") * shard_rows
        local_ids = token_ids - row_offset
        owned = (local_ids >= 0) & (local_ids < shard_rows)
        looked_up = jnp.take(table_shard, jnp.clip(local_ids, 0, shard_rows - 1), axis=0, mode="clip")
        partial_rows = jnp.where(owned[:, None], looked_up, jnp.zeros((), jnp.bfloat16))
        embedded = lax.psum_scatter(partial_rows, "tp", scatter_dimension=0, tiled=True)
        normed = rms_norm(embedded, norm_gain)
        normed_all = lax.all_gather(normed, "tp", axis=0, tiled=True)
        pre_act = jnp.dot(normed_all, w_in_shard, preferred_element_type=jnp.float32).astype(jnp.bfloat16)
        activated = jax.nn.gelu(pre_act.astype(jnp.float32), approximate=True).astype(jnp.bfloat16)
        mlp_part = jnp.dot(activated, w_out_shard, preferred_element_type=jnp.float32)
        mlp_sum = lax.psum_scatter(mlp_part, "tp", scatter_dimension=0, tiled=True)
        return (embedded.astype(jnp.float32) + mlp_sum).astype(jnp.bfloat16)

    return jax.shard_map(
        device_step,
        mesh=mesh,
        in_specs=(P("dp"), P("tp", None), P(), P(None, "tp"), P("tp", None)),
        out_specs=P(("dp", "tp"), None),
        check_vma=False,
    )
```

profile of v0, /device:TPU:0, one launch (start us, length us, event | category | flops | bytes accessed | tf_op | source)
XLA Modules:
  0.0 864.1 jit_solution(6147110704481472379)
XLA Ops:
  6.5 0.0 reduce-scatter.3.cloned.1.call-start
  6.5 0.7 compare_and_fusion
  7.3 0.7 clamp_clamp_fusion
  8.0 161.6 %gather_fusion = bf16[4096,2048]{1,0:T(8,128)(2,1)} fusion(bf16[64000,2048]{1,0:T(8,128)(2,1)} %param.6, s32[4096]{0:T(1024)S(1)} %clamp_clamp_fusion), kind=kCustom, calls=%fused_computation | custom fusion | bytes 33570816 | tf_op jit(solution)/shard_map/jit(_take)/gather | solution.py:21
  169.6 14.5 %broadcast_select_fusion = bf16[4096,2048]{1,0:T(8,128)(2,1)} fusion(bf16[4096,2048]{1,0:T(8,128)(2,1)} %gather_fusion, pred[4096]{0:T(1024)(128)(4,1)S(1)} %compare_and_fusion), kind=kLoop, calls=%fused_computation.12 | loop fusion | flops 8388608 | bytes 33558528 | tf_op jit(solution)/shard_map/jit(_where)/select_n | solution.py:22
  184.1 0.0 copy-start
  184.1 0.0 reduce-scatter.3.cloned.1.call-update
  184.1 0.0 all-gather.2.cloned.1.call-start
  184.2 0.6 copy-done
  184.8 155.9 %reduce-scatter.3.cloned.1.call-done = bf16[1024,2048]{1,0:T(8,128)(2,1)} async-done(((bf16[4096,2048]{1,0:T(8,128)(2,1)}), bf16[1024,2048]{1,0:T(8,128)(2,1)}) %reduce-scatter.3.cloned.1.call-update) | async-done | bytes 4194320 | tf_op jit(solution)/shard_map/reduce_scatter | solution.py:23
  340.7 3.1 fusion.8
  343.7 5.2 fusion.10
  349.0 0.0 all-gather.2.cloned.1.call-update
  349.0 0.2 reduce-scatter.5.cloned.1.call-start
  349.2 104.1 %all-gather.2.cloned.1.call-done = bf16[4096,2048]{1,0:T(8,128)(2,1)} async-done(((bf16[1024,2048]{1,0:T(8,128)(2,1)}), bf16[4096,2048]{1,0:T(8,128)(2,1)}) %all-gather.2.cloned.1.call-update) | async-done | bytes 16777232 | tf_op jit(solution)/shard_map/all_gather | solution.py:25
  453.4 78.4 %fusion.16 = bf16[4096,4096]{1,0:T(8,128)(2,1)} fusion(bf16[4096,2048]{1,0:T(8,128)(2,1)} %all-gather.2.cloned.1.call-done, bf16[2048,4096]{1,0:T(8,128)(2,1)} %param.8), kind=kOutput, calls=%fused_computation.27 | convolution fusion | flops 68719476736 | bytes 67108864 | tf_op jit(solution)/shard_map/dot_general | solution.py:26
  531.8 91.3 %fusion.6 = f32[4096,2048]{1,0:T(8,128)} fusion(bf16[4096,2048]{1,0:T(8,128)(2,1)} %param.9, bf16[4096,4096]{1,0:T(8,128)(2,1)} %fusion.16), kind=kOutput, calls=%fused_computation.11 | convolution fusion | flops 68887248896 | bytes 83886080 | tf_op jit(solution)/shard_map/dot_general | solution.py:28
  623.1 0.0 reduce-scatter.5.cloned.1.call-update
  623.1 226.2 %reduce-scatter.5.cloned.1.call-done = f32[1024,2048]{1,0:T(8,128)} async-done(((f32[4096,2048]{1,0:T(8,128)}), f32[1024,2048]{1,0:T(8,128)}) %reduce-scatter.5.cloned.1.call-update) | async-done | bytes 8388624 | tf_op jit(solution)/shard_map/reduce_scatter | solution.py:29
  849.3 8.3 fusion.11
  (2 shorter events, 0.0 us)
Async XLA Ops:
  6.5 334.1 %reduce-scatter.3.cloned.1.call-start = ((), (), s32[]{:S(2)}) async-start(), calls=%async_computation.2 | async-start | bytes 20971520 | tf_op jit(solution)/shard_map/reduce_scatter | solution.py:23
  184.1 0.7 copy-start
  184.1 269.2 %all-gather.2.cloned.1.call-start = ((), (), s32[]{:S(2)}) async-start(), calls=%async_computation.3 | async-start | bytes 20971520 | tf_op jit(solution)/shard_map/all_gather | solution.py:25
  349.0 500.3 %reduce-scatter.5.cloned.1.call-start = ((), (), s32[]{:S(2)}) async-start(), calls=%async_computation.4 | async-start | bytes 41943040 | tf_op jit(solution)/shard_map/reduce_scatter | solution.py:29
Sparse Core Ops, SparseCore 0:
  184.2 156.3 reduce-scatter.2
  349.1 104.1 all-gather.1
  623.2 226.0 reduce-scatter.4
where the time goes:
time: 868 us; the launch traced here: 864 us
  waiting for transfers between devices  486 us (56%)
  matrix products  170 us (20%)
  local copies, waits for them, and re-layouts  162 us (19%)
  other arithmetic  32.6 us (4%)
  between operations  13.1 us (2%)
    reduce_scatter x1, waiting for transfers between devices, device_step(): mlp_sum = lax.psum_scatter(mlp_part, 'tp', scatter_dimension=0, tiled=True)  226 us
    gather x1, local copies, waits for them, and re-layouts, device_step(): jnp.take(table_shard, jnp.clip(local_ids, 0, shard_rows - 1), axis=0, mod...  162 us
    reduce_scatter x1, waiting for transfers between devices, device_step(): lax.psum_scatter(partial_rows, 'tp', scatter_dimension=0, tiled=True)  156 us
    all_gather x1, waiting for transfers between devices, device_step(): normed_all = lax.all_gather(normed, 'tp', axis=0, tiled=True)  104 us
    dot_general x1, matrix products, device_step(): jnp.dot(activated, w_out_shard, preferred_element_type=jnp.float32)  91.3 us
    dot_general x1, matrix products, device_step(): jnp.dot(normed_all, w_in_shard, preferred_element_type=jnp.float32)  78.4 us
  transfers between devices with their start and end apart: 3, of which 3 were waited for; matrix products, arithmetic and copies ran while one was open for 0% of the time, Pallas kernels for 0%

commit v1 on v0

v1 whole, which is shorter than its diff:
```python
import functools

import jax
import jax.numpy as jnp
from jax import lax
from jax.experimental import pallas as pl
from jax.experimental.pallas import tpu as pltpu
from jax.sharding import PartitionSpec as P

RMS_EPS = 1e-6
TILE = 32
SLOTS = 6
PIECE = 128
CHUNK = 512
WIDTH = 512
MESH = pl.DeviceIdType.MESH


def gather_kernel(tiles, span_ref, ids_ref, pick_ref, table_ref, out_ref, slabs, rows, steps, slab_sem, row_sem):
    n_spans = span_ref.shape[0] // 2
    total = 0
    for span in range(n_spans):
        first, last = span_ref[2 * span], span_ref[2 * span + 1]

        def note(t, _, span=span, first=first, total=total):
            steps[total + t - first] = span * tiles + t
            return 0

        lax.fori_loop(first, last, note, 0)
        total = total + last - first

    def fetch(step):
        slot = lax.rem(step, SLOTS)
        base = steps[step] * TILE
        for j in range(TILE):
            slab = lax.shift_right_logical(ids_ref[base + j], 3)
            pltpu.make_async_copy(
                table_ref.at[slab], slabs.at[slot, pl.ds(8 * j, 8), :], slab_sem.at[slot]
            ).start()

    for step in range(SLOTS - 1):
        @pl.when(step < total)
        def _(step=step):
            fetch(step)

    def out_copy(step):
        slot = lax.rem(step, 2)
        return pltpu.make_async_copy(
            rows.at[slot], out_ref.at[pl.ds(steps[step] * TILE, TILE), :], row_sem.at[slot]
        )

    def work(step, _):
        @pl.when(step + SLOTS - 1 < total)
        def _():
            fetch(step + SLOTS - 1)

        slot = lax.rem(step, SLOTS)
        pltpu.make_async_copy(slabs.at[slot], slabs.at[slot], slab_sem.at[slot]).wait()
        base = pl.multiple_of(steps[step] * TILE, TILE)
        col = lax.broadcasted_iota(jnp.int32, (TILE, 8 * TILE), 1)
        want = pick_ref[pl.ds(base, TILE), :] + 8 * lax.broadcasted_iota(jnp.int32, (TILE, 8 * TILE), 0)
        pick = (col == want).astype(jnp.float32).astype(jnp.bfloat16)

        @pl.when(step >= 2)
        def _():
            out_copy(step - 2).wait()

        rows[lax.rem(step, 2)] = jnp.dot(
            pick, slabs[slot], preferred_element_type=jnp.float32
        ).astype(jnp.bfloat16)
        out_copy(step).start()
        return 0

    lax.fori_loop(0, total, work, 0)
    for back in (2, 1):
        @pl.when(total >= back)
        def _(back=back):
            out_copy(total - back).wait()


def gather_rows(table_shard, spans, ids, picks, cap):
    n_rows, dim = ids.shape[0], table_shard.shape[1]
    return pl.pallas_call(
        functools.partial(gather_kernel, cap // TILE),
        out_shape=jax.ShapeDtypeStruct((n_rows, dim), jnp.bfloat16),
        in_specs=[
            pl.BlockSpec(memory_space=pltpu.SMEM),
            pl.BlockSpec(memory_space=pltpu.SMEM),
            pl.BlockSpec(memory_space=pltpu.VMEM),
            pl.BlockSpec(memory_space=pl.ANY),
        ],
        out_specs=pl.BlockSpec(memory_space=pl.ANY),
        scratch_shapes=[
            pltpu.VMEM((SLOTS, 8 * TILE, dim), jnp.bfloat16),
            pltpu.VMEM((2, TILE, dim), jnp.bfloat16),
            pltpu.SMEM((n_rows // TILE,), jnp.int32),
            pltpu.SemaphoreType.DMA((SLOTS,)),
            pltpu.SemaphoreType.DMA((2,)),
        ],
        compiler_params=pltpu.CompilerParams(vmem_limit_bytes=40 << 20),
        name="gather_rows",
    )(spans, ids, picks, table_shard.reshape(-1, 8, dim))


def prepare(token_ids, shard_rows, cap):
    me = lax.axis_index("tp")
    chip = me // 2
    other, partner = me ^ 2, me ^ 1
    blocks = jnp.stack([other ^ 1, partner, other, me])
    ids = jnp.take(token_ids.reshape(4, -1), blocks, axis=0)
    n_tok = ids.shape[1]
    owner = ids // shard_rows
    is_of = (owner[:, None, :] == jnp.arange(4)[None, :, None])
    upto = (lax.broadcasted_iota(jnp.int32, (n_tok, n_tok), 0) <= lax.broadcasted_iota(jnp.int32, (n_tok, n_tok), 1))
    counts_to = jnp.dot(
        is_of.reshape(16, n_tok).astype(jnp.bfloat16), upto.astype(jnp.bfloat16), preferred_element_type=jnp.float32
    ).astype(jnp.int32).reshape(4, 4, n_tok)
    counts = counts_to[:, :, -1]
    starts = jnp.stack([jnp.zeros_like(counts[:, 0]), counts[:, 0], jnp.zeros_like(counts[:, 0]), counts[:, 2]], axis=1)
    place = jnp.sum(jnp.where(is_of, counts_to - 1 + starts[:, :, None], 0), axis=1)

    my_start = jnp.take(starts, me, axis=1)
    my_end = my_start + jnp.take(counts, me, axis=1)
    spans = jnp.stack([my_start // TILE, (my_end + TILE - 1) // TILE], axis=1)
    spans = jnp.where((my_end > my_start)[:, None], spans, 0).reshape(8)
    mine = owner == me
    slot = lax.broadcasted_iota(jnp.int32, (4, n_tok, cap), 2)
    hit = (place[:, :, None] == slot) & mine[:, :, None]
    ids_at = jnp.max(jnp.where(hit, (ids - me * shard_rows)[:, :, None], 0), axis=1).reshape(-1)
    picks = (ids_at & 7)[:, None]

    ours = (owner // 2) == chip
    from_ours = jnp.where(ours, place, -1)[2:, :, None]
    from_other = jnp.where(ours, -1, place)[2:, :, None]
    first = jnp.take(counts, 2 * chip, axis=1)[2:, None]
    both = first + jnp.take(counts, 2 * chip + 1, axis=1)[2:, None]
    pos = lax.broadcasted_iota(jnp.int32, (2, cap), 1)
    is_core0 = pos < first
    source = jnp.where(pos < both, jnp.where(is_core0 == (me % 2 == 0), 0, 1), 2)[:, :, None]
    return spans, ids_at, picks, from_ours, from_other, source


def block_kernel(
    cap, gain_ref, ours_ref, other_ref, source_ref, rows_ref, w1_ref, w2_ref,
    out_ref, w1p_ref, w2p_ref, sums_ref,
    inbox, ours_rows, normed, kept, acc, w1_buf, w2_buf, sum_buf, out_buf,
    pair_send, pair_recv, load_sem, w_send, w_recv, ready, x_send, x_recv, w_sem, s_send, s_recv, r_sem, o_sem,
):
    me, dp = lax.axis_index("tp"), lax.axis_index("dp")
    core = lax.rem(me, 2)
    partner = me + 1 - 2 * core
    other = lax.rem(me + 2, 4)
    dim = gain_ref.shape[1]
    n_tok = out_ref.shape[0]
    width = w1_ref.shape[1]
    w_steps = width // WIDTH
    n_chunks = n_tok // CHUNK
    n_pieces = n_tok // PIECE

    barrier = pltpu.get_barrier_semaphore()
    for peer in (partner, other):
        pl.semaphore_signal(barrier, inc=1, device_id=(dp, peer), device_id_type=MESH)
    pl.semaphore_wait(barrier, 2)

    def remote(src, dst, send, recv, peer):
        return pltpu.make_async_remote_copy(
            src_ref=src, dst_ref=dst, send_sem=send, recv_sem=recv, device_id=(dp, peer), device_id_type=MESH
        )

    pair = [
        remote(rows_ref.at[pl.ds((1 - p) * cap, cap), :], inbox.at[p], pair_send.at[p], pair_recv.at[p], partner)
        for p in range(2)
    ]
    loads = [
        pltpu.make_async_copy(rows_ref.at[pl.ds((3 - p) * cap, cap), :], ours_rows.at[1 - p], load_sem.at[p])
        for p in range(2)
    ]
    weights = [
        remote(w1_ref, w1p_ref, w_send.at[0], w_recv.at[0], partner),
        remote(w2_ref, w2p_ref, w_send.at[1], w_recv.at[1], partner),
    ]
    for p in range(2):
        pair[p].start()
        loads[p].start()
    for copy in weights:
        copy.start()

    def fetch_weights(step, slot, start):
        @pl.when(step < w_steps)
        def _():
            cols = pl.ds(pl.multiple_of(step * WIDTH, WIDTH), WIDTH)
            start(pltpu.make_async_copy(w1_ref.at[:, cols], w1_buf.at[slot], w_sem.at[0, slot]))
            start(pltpu.make_async_copy(w2_ref.at[cols, :], w2_buf.at[slot], w_sem.at[1, slot]))

        @pl.when(step >= w_steps)
        def _():
            cols = pl.ds(pl.multiple_of((step - w_steps) * WIDTH, WIDTH), WIDTH)
            start(pltpu.make_async_copy(w1p_ref.at[:, cols], w1_buf.at[slot], w_sem.at[0, slot]))
            start(pltpu.make_async_copy(w2p_ref.at[cols, :], w2_buf.at[slot], w_sem.at[1, slot]))

    fetch_weights(0, 0, lambda copy: copy.start())

    cross = [
        remote(ours_rows.at[1 - p], inbox.at[p], x_send.at[p], x_recv.at[p], other) for p in range(2)
    ]
    for p in range(2):
        b = 1 - p
        loads[p].wait()
        pair[p].wait_recv()

        @pl.loop(0, cap // TILE)
        def _(t, p=p, b=b):
            span = pl.ds(pl.multiple_of(t * TILE, TILE), TILE)
            source = source_ref[b, span, :]
            mine = ours_rows[b, span, :].astype(jnp.float32)
            theirs = inbox[p, span, :].astype(jnp.float32)
            ours_rows[b, span, :] = jnp.where(
                source == 0, mine, jnp.where(source == 1, theirs, 0.0)
            ).astype(jnp.bfloat16)

        pl.semaphore_signal(ready.at[p], inc=1, device_id=(dp, other), device_id_type=MESH)
        pl.semaphore_wait(ready.at[p], 1)
        cross[p].start()

    gain = gain_ref[...].astype(jnp.float32)

    def send_sums(piece):
        span = pl.ds(pl.multiple_of(piece * PIECE, PIECE), PIECE)
        return remote(acc.at[span, :], sums_ref.at[span, :], s_send.at[piece], s_recv.at[piece], other)

    @pl.loop(0, 2)
    def _(b):
        remote(ours_rows.at[b], inbox.at[b], x_send.at[b], x_recv.at[b], other).wait_recv()

        @pl.loop(0, n_tok // 256)
        def _(t):
            span = pl.ds(pl.multiple_of(t * 256, 256), 256)
            slot = lax.broadcasted_iota(jnp.int32, (256, cap), 1)
            pick_ours = (slot == ours_ref[b, span, :]).astype(jnp.float32).astype(jnp.bfloat16)
            pick_other = (slot == other_ref[b, span, :]).astype(jnp.float32).astype(jnp.bfloat16)
            rows = jnp.dot(pick_ours, ours_rows[b], preferred_element_type=jnp.float32) + jnp.dot(
                pick_other, inbox[b], preferred_element_type=jnp.float32
            )
            kept[span, :] = rows.astype(jnp.bfloat16)
            inv_rms = lax.rsqrt(jnp.mean(rows * rows, axis=-1, keepdims=True) + RMS_EPS)
            normed[span, :] = (rows * inv_rms * gain).astype(jnp.bfloat16)

        @pl.loop(0, n_chunks)
        def _(chunk):
            tok = pl.ds(pl.multiple_of(chunk * CHUNK, CHUNK), CHUNK)
            out_rows = pl.ds(pl.multiple_of(b * n_tok + chunk * CHUNK, CHUNK), CHUNK)
            acc[out_rows, :] = jnp.zeros((CHUNK, dim), jnp.float32)

            @pl.loop(0, 2 * w_steps)
            def _(w):
                step = (b * n_chunks + chunk) * 2 * w_steps + w
                slot = lax.rem(step, 2)
                fetch_weights(w, slot, lambda copy: copy.wait())

                @pl.when(step == w_steps - 1)
                def _():
                    for copy in weights:
                        copy.wait_recv()

                @pl.when(step + 1 < 2 * n_chunks * 2 * w_steps)
                def _():
                    fetch_weights(lax.rem(step + 1, 2 * w_steps), 1 - slot, lambda copy: copy.start())

                parts = []
                for half in range(2):
                    cols = pl.ds(half * (WIDTH // 2), WIDTH // 2)
                    z = jnp.dot(normed[tok, :], w1_buf[slot, :, cols], preferred_element_type=jnp.float32)
                    z = z.astype(jnp.bfloat16).astype(jnp.float32)
                    inner = 0.7978845608028654 * (z + 0.044715 * (z * z * z))
                    parts.append((0.5 * z * (1.0 + jnp.tanh(inner))).astype(jnp.bfloat16))
                hidden = jnp.concatenate(parts, axis=1)
                for half in range(2):
                    cols = pl.ds(half * (dim // 2), dim // 2)
                    acc[out_rows, cols] += jnp.dot(
                        hidden, w2_buf[slot, :, cols], preferred_element_type=jnp.float32
                    )

            @pl.when(b == 0)
            def _():
                for q in range(CHUNK // PIECE):
                    send_sums(chunk * (CHUNK // PIECE) + q).start()

    def take_sums(piece, slot):
        span = pl.ds(pl.multiple_of(piece * PIECE, PIECE), PIECE)
        return pltpu.make_async_copy(sums_ref.at[span, :], sum_buf.at[slot], r_sem.at[slot])

    def put_out(piece, slot):
        span = pl.ds(pl.multiple_of(piece * PIECE, PIECE), PIECE)
        return pltpu.make_async_copy(out_buf.at[slot], out_ref.at[span, :], o_sem.at[slot])

    @pl.loop(0, n_pieces)
    def _(piece):
        slot = lax.rem(piece, 2)
        send_sums(piece).wait_recv()
        take = take_sums(piece, slot)
        take.start()
        take.wait()

        @pl.when(piece >= 2)
        def _():
            put_out(piece - 2, slot).wait()

        span = pl.ds(pl.multiple_of(piece * PIECE, PIECE), PIECE)
        own = pl.ds(pl.multiple_of(n_tok + piece * PIECE, PIECE), PIECE)
        total = acc[own, :] + sum_buf[slot]
        out_buf[slot] = (kept[span, :].astype(jnp.float32) + total).astype(jnp.bfloat16)
        put_out(piece, slot).start()

    put_out(n_pieces - 2, lax.rem(n_pieces - 2, 2)).wait()
    put_out(n_pieces - 1, lax.rem(n_pieces - 1, 2)).wait()

    for copy in pair + weights + cross:
        copy.wait_send()

    @pl.loop(0, n_pieces)
    def _(piece):
        send_sums(piece).wait_send()


def mlp_block(gain, from_ours, from_other, source, rows, w_in, w_out, n_tok, cap):
    dim, width = w_in.shape
    any_spec, vmem = pl.BlockSpec(memory_space=pl.ANY), pl.BlockSpec(memory_space=pltpu.VMEM)
    dma = pltpu.SemaphoreType.DMA
    n_pieces = n_tok // PIECE
    flops = 2 * (2 * n_tok) * dim * (2 * width) * 2
    return pl.pallas_call(
        functools.partial(block_kernel, cap),
        out_shape=[
            jax.ShapeDtypeStruct((n_tok, dim), jnp.bfloat16),
            jax.ShapeDtypeStruct(w_in.shape, w_in.dtype),
            jax.ShapeDtypeStruct(w_out.shape, w_out.dtype),
            jax.ShapeDtypeStruct((n_tok, dim), jnp.float32),
        ],
        in_specs=[vmem, vmem, vmem, vmem, any_spec, any_spec, any_spec],
        out_specs=[any_spec] * 4,
        scratch_shapes=[
            pltpu.VMEM((2, cap, dim), jnp.bfloat16),
            pltpu.VMEM((2, cap, dim), jnp.bfloat16),
            pltpu.VMEM((n_tok, dim), jnp.bfloat16),
            pltpu.VMEM((n_tok, dim), jnp.bfloat16),
            pltpu.VMEM((2 * n_tok, dim), jnp.float32),
            pltpu.VMEM((2, dim, WIDTH), jnp.bfloat16),
            pltpu.VMEM((2, WIDTH, dim), jnp.bfloat16),
            pltpu.VMEM((2, PIECE, dim), jnp.float32),
            pltpu.VMEM((2, PIECE, dim), jnp.bfloat16),
            dma((2,)), dma((2,)), dma((2,)), dma((2,)), dma((2,)),
            pltpu.SemaphoreType.REGULAR((2,)),
            dma((2,)), dma((2,)), dma((2, 2)), dma((n_pieces,)), dma((n_pieces,)), dma((2,)), dma((2,)),
        ],
        compiler_params=pltpu.CompilerParams(
            collective_id=0, has_side_effects=True, vmem_limit_bytes=67043328
        ),
        cost_estimate=pl.CostEstimate(flops=flops, bytes_accessed=1 << 28, transcendentals=0),
        name="mlp_block",
    )(gain, from_ours, from_other, source, rows, w_in, w_out)


def solution(mesh):
    def device_step(token_ids, table_shard, norm_gain, w_in_shard, w_out_shard):
        n_tok = token_ids.shape[0] // 4
        cap = n_tok
        spans, ids_at, picks, from_ours, from_other, source = prepare(token_ids, table_shard.shape[0], cap)
        rows = gather_rows(table_shard, spans, ids_at, picks, cap)
        return mlp_block(
            norm_gain[None, :], from_ours, from_other, source, rows, w_in_shard, w_out_shard, n_tok, cap
        )[0]

    return jax.shard_map(
        device_step,
        mesh=mesh,
        in_specs=(P("dp"), P("tp", None), P(), P(None, "tp"), P("tp", None)),
        out_specs=P(("dp", "tp"), None),
        check_vma=False,
    )
```

time: 868 us -> 428 us (0.49)
  waiting for transfers between devices: 486 us -> 0 us
  Pallas kernels: 0 us -> 407 us
  matrix products: 170 us -> 0.37 us
  local copies, waits for them, and re-layouts: 162 us -> 11.4 us
  other arithmetic: 32.6 us -> 7.47 us
  between operations: 13.1 us -> 0.12 us
    pallas_call x0 -> x2, Pallas kernels: none -> 407 us  [the longest x1 377 us: mlp_block(): pl.pallas_call(functools.partial(block_kernel, cap), out_shape=[jax.Shape...]
    reduce_scatter x2 -> x0, waiting for transfers between devices: 382 us -> none  [the longest x1 226 us: device_step(): mlp_sum = lax.psum_scatter(mlp_part, 'tp', scatter_dimension=0, tiled=True)]
    dot_general x2 -> x1, matrix products: 170 us -> 0.37 us  [prepare(): jnp.dot(is_of.reshape(16, n_tok).astype(jnp.bfloat16), upto.astype(jnp.bf...]
    gather x1, local copies, waits for them, and re-layouts: 162 us -> 0.56 us  [prepare(): ids = jnp.take(token_ids.reshape(4, -1), blocks, axis=0)]
    all_gather x1 -> x0, waiting for transfers between devices: 104 us -> none  [device_step(): normed_all = lax.all_gather(normed, 'tp', axis=0, tiled=True)]
    convert_element_type x3 -> x0, other arithmetic: 13.5 us -> none  [the longest x1 8.29 us: device_step(): return (embedded.astype(jnp.float32) + mlp_sum).astype(jnp.bfloat16)]
    select_n x1 -> x5, other arithmetic: 14.5 us -> 1.84 us  [the longest x1 1.3 us: prepare(): jnp.where(pos < both, jnp.where(is_core0 == (me % 2 == 0), 0, 1), 2)]
  transfers between devices with their start and end apart: 3 -> 0, of which waited for: 3 -> 0; matrix products, arithmetic and copies ran while one was open for 0% -> 0% of each run, Pallas kernels for 0% -> 0%
where the time goes in v1:
time: 428 us; the launch traced here: 426 us
  Pallas kernels  407 us (95%)
  local copies, waits for them, and re-layouts  11.4 us (3%)
  other arithmetic  7.47 us (2%)
    pallas_call x1, Pallas kernels, mlp_block(): pl.pallas_call(functools.partial(block_kernel, cap), out_shape=[jax.Shape...  377 us
    pallas_call x1, Pallas kernels, gather_rows(): pl.pallas_call(functools.partial(gather_kernel, cap // TILE), out_shape=j...  29.7 us

profile of v1, /device:TPU:0, one launch (start us, length us, event | category | flops | bytes accessed | tf_op | source)
XLA Modules:
  0.0 426.1 jit_solution(8348931403482865015)
XLA Ops:
  0.0 0.1 compare_and_fusion
  0.1 0.1 pad_add_fusion.1
  0.2 0.1 copy.26
  0.3 0.1 fusion.12
  0.4 0.1 eq.73
  0.5 1.3 broadcast_in_dim.80.gain_ref
  1.8 0.7 reshape.345
  2.5 0.6 gather_fusion
  3.1 0.1 select_subtract_fusion
  3.1 0.1 broadcast_compare_fusion
  3.3 0.4 fusion.2
  3.7 0.1 slice.37
  3.8 0.1 copy.34
  3.9 0.2 select_reduce_fusion.2
  4.2 0.1 pad_add_fusion
  4.2 0.1 select_reduce_fusion.1
  4.4 5.0 %select_reduce_fusion = s32[4,1024]{1,0:T(4,128)S(1)} fusion(s32[4,1024]{1,0:T(4,128)S(1)} %select_subtract_fusion, s32[4,1024]{1,0:T(4,128)S(1)} %select_reduce_fusion.1, pred[4,1024]{1,0:T(4,128)(4,1)S(1)} %get-tuple-element.22), kind=kLoop, calls=%fused_computation.1 | loop fusion | flops 16773120 | bytes 53248 | tf_op jit(solution)/shard_map/reduce_max | solution.py:129
  9.3 0.2 select_reduce_fusion.3
  9.5 0.1 slice_add_fusion
  9.6 0.1 copy.30
  9.7 0.1 select_n.132.span_ref
  9.9 1.4 copy.33.other_ref
  11.2 1.3 select_select_fusion.source_ref
  12.5 1.3 copy.32.ours_ref
  13.9 0.6 copy.37
  14.5 29.7 %gather_rows.1.rows_ref = bf16[4096,2048]{1,0:T(8,128)(2,1)} custom-call(s32[8]{0:T(128)S(1)} %select_n.132.span_ref, s32[4096]{0:T(1024)S(1)} %bitcast.28, s32[4096,1]{1,0:T(8,128)S(1)} %bitcast.27, bf16[8000,8,2048]{2,1,0:T(8,128)(2,1)} %bitcast.13.table_ref), custom_call_target="tpu_custom_call" | custom-call | tf_op jit(solution)/shard_map/gather_rows/pallas_call | solution.py:83
  44.3 377.1 %mlp_block.1 = (bf16[1024,2048]{1,0:T(8,128)(2,1)}, bf16[2048,4096]{1,0:T(8,128)(2,1)}, bf16[4096,2048]{1,0:T(8,128)(2,1)}, f32[1024,2048]{1,0:T(8,128)}) custom-call(bf16[1,2048]{1,0:T(2,128)(2,1)} %broadcast_in_dim.80.gain_ref, s32[2,1024,1]{2,1,0:T(8,128)} %copy.32.ours_ref, s32[2,1024,1]{2,1,0:T(8,128)} %copy.33.other_ref, ...), custom_call_target="tpu_custom_call" | custom-call | flops 137438953472 | bytes 268435456 | tf_op jit(solution)/shard_map/mlp_block/pallas_call | solution.py:331
  421.3 4.8 %copy.41 = bf16[1024,2048]{1,0:T(8,128)(2,1)} copy(bf16[1024,2048]{1,0:T(8,128)(2,1)} %get-tuple-element.7) | data formatting | bytes 8388608
  (14 shorter events, 0.2 us)

commit v2 on v1

--- a/solution.py
+++ b/solution.py
@@ -13,6 +13,7 @@
 PIECE = 128
 CHUNK = 512
 WIDTH = 512
+PACKED = 704
 MESH = pl.DeviceIdType.MESH
 
 
@@ -98,6 +99,7 @@
             pltpu.SemaphoreType.DMA((2,)),
         ],
         compiler_params=pltpu.CompilerParams(vmem_limit_bytes=40 << 20),
+        cost_estimate=pl.CostEstimate(flops=1 << 34, bytes_accessed=1 << 26, transcendentals=0),
         name="gather_rows",
     )(spans, ids, picks, table_shard.reshape(-1, 8, dim))
 
@@ -137,11 +139,12 @@
     pos = lax.broadcasted_iota(jnp.int32, (2, cap), 1)
     is_core0 = pos < first
     source = jnp.where(pos < both, jnp.where(is_core0 == (me % 2 == 0), 0, 1), 2)[:, :, None]
-    return spans, ids_at, picks, from_ours, from_other, source
+    most = jnp.max(jnp.stack([counts[:, 0] + counts[:, 1], counts[:, 2] + counts[:, 3]]))
+    return spans, ids_at, picks, from_ours, from_other, source, most
 
 
 def block_kernel(
-    cap, gain_ref, ours_ref, other_ref, source_ref, rows_ref, w1_ref, w2_ref,
+    cap, stride, gain_ref, ours_ref, other_ref, source_ref, rows_ref, w1_ref, w2_ref,
     out_ref, w1p_ref, w2p_ref, sums_ref,
     inbox, ours_rows, normed, kept, acc, w1_buf, w2_buf, sum_buf, out_buf,
     pair_send, pair_recv, load_sem, w_send, w_recv, ready, x_send, x_recv, w_sem, s_send, s_recv, r_sem, o_sem,
@@ -168,11 +171,11 @@
         )
 
     pair = [
-        remote(rows_ref.at[pl.ds((1 - p) * cap, cap), :], inbox.at[p], pair_send.at[p], pair_recv.at[p], partner)
+        remote(rows_ref.at[pl.ds((1 - p) * stride, cap), :], inbox.at[p], pair_send.at[p], pair_recv.at[p], partner)
         for p in range(2)
     ]
     loads = [
-        pltpu.make_async_copy(rows_ref.at[pl.ds((3 - p) * cap, cap), :], ours_rows.at[1 - p], load_sem.at[p])
+        pltpu.make_async_copy(rows_ref.at[pl.ds((3 - p) * stride, cap), :], ours_rows.at[1 - p], load_sem.at[p])
         for p in range(2)
     ]
     weights = [
@@ -322,14 +325,15 @@
         send_sums(piece).wait_send()
 
 
-def mlp_block(gain, from_ours, from_other, source, rows, w_in, w_out, n_tok, cap):
+def mlp_block(cap, collective_id, gain, from_ours, from_other, source, rows, w_in, w_out):
+    n_tok = rows.shape[0] // 4
     dim, width = w_in.shape
     any_spec, vmem = pl.BlockSpec(memory_space=pl.ANY), pl.BlockSpec(memory_space=pltpu.VMEM)
     dma = pltpu.SemaphoreType.DMA
     n_pieces = n_tok // PIECE
     flops = 2 * (2 * n_tok) * dim * (2 * width) * 2
     return pl.pallas_call(
-        functools.partial(block_kernel, cap),
+        functools.partial(block_kernel, cap, n_tok),
         out_shape=[
             jax.ShapeDtypeStruct((n_tok, dim), jnp.bfloat16),
             jax.ShapeDtypeStruct(w_in.shape, w_in.dtype),
@@ -353,22 +357,28 @@
             dma((2,)), dma((2,)), dma((2, 2)), dma((n_pieces,)), dma((n_pieces,)), dma((2,)), dma((2,)),
         ],
         compiler_params=pltpu.CompilerParams(
-            collective_id=0, has_side_effects=True, vmem_limit_bytes=67043328
+            collective_id=collective_id, has_side_effects=True, vmem_limit_bytes=67043328
         ),
         cost_estimate=pl.CostEstimate(flops=flops, bytes_accessed=1 << 28, transcendentals=0),
         name="mlp_block",
-    )(gain, from_ours, from_other, source, rows, w_in, w_out)
+    )(gain, from_ours, from_other, source[:, :cap], rows, w_in, w_out)[0]
 
 
 def solution(mesh):
+    swap = [(0, 1), (1, 0)]
+
     def device_step(token_ids, table_shard, norm_gain, w_in_shard, w_out_shard):
         n_tok = token_ids.shape[0] // 4
-        cap = n_tok
-        spans, ids_at, picks, from_ours, from_other, source = prepare(token_ids, table_shard.shape[0], cap)
-        rows = gather_rows(table_shard, spans, ids_at, picks, cap)
-        return mlp_block(
-            norm_gain[None, :], from_ours, from_other, source, rows, w_in_shard, w_out_shard, n_tok, cap
-        )[0]
+        *lists, from_ours, from_other, source, most = prepare(token_ids, table_shard.shape[0], n_tok)
+        most = jnp.full((8, 128), most, jnp.int32)
+        most = jnp.max(jnp.maximum(most, lax.ppermute(most, "dp", swap)))
+        rows = gather_rows(table_shard, *lists, n_tok)
+        return lax.cond(
+            most <= PACKED,
+            functools.partial(mlp_block, PACKED, 0),
+            functools.partial(mlp_block, n_tok, 1),
+            norm_gain[None, :], from_ours, from_other, source, rows, w_in_shard, w_out_shard,
+        )
 
     return jax.shard_map(
         device_step,

time: 428 us -> 377 us (0.88)
  Pallas kernels: 407 us -> 349 us
    pallas_call x1, Pallas kernels: 377 us -> 318 us  [mlp_block(): pl.pallas_call(functools.partial(block_kernel, cap, n_tok), out_shape=[ja...]
  transfers between devices with their start and end apart: 0 -> 1, of which waited for: 0 -> 0; matrix products, arithmetic and copies ran while one was open for 0% -> 2% of each run, Pallas kernels for 0% -> 8%
where the time goes in v2:
time: 377 us; the launch traced here: 376 us
  Pallas kernels  349 us (93%)
  local copies, waits for them, and re-layouts  12.8 us (3%)
  other arithmetic  8.66 us (2%)
    pallas_call x1, Pallas kernels, mlp_block(): pl.pallas_call(functools.partial(block_kernel, cap, n_tok), out_shape=[ja...  318 us
    pallas_call x1, Pallas kernels, gather_rows(): pl.pallas_call(functools.partial(gather_kernel, cap // TILE), out_shape=j...  30.7 us
  transfers between devices with their start and end apart: 1, of which 0 were waited for; matrix products, arithmetic and copies ran while one was open for 2% of the time, Pallas kernels for 8%

profile of v2, /device:TPU:0, one launch (start us, length us, event | category | flops | bytes accessed | tf_op | source)
XLA Modules:
  0.0 376.0 jit_solution(11812761415058061515)
XLA Ops:
  0.0 0.1 pad_add_fusion.1
  0.1 0.1 copy.31
  0.2 0.1 fusion.12
  0.3 0.1 eq.69
  0.4 0.7 reshape.381
  1.1 0.6 gather_fusion
  1.7 0.1 compare_and_fusion
  1.8 0.1 broadcast_compare_fusion
  1.9 0.4 fusion.2
  2.3 0.1 slice.50
  2.4 0.1 copy.41
  2.5 0.8 fusion.15
  4.6 3.4 collective-permute-start
  8.1 0.1 pad_add_fusion
  8.1 0.1 select_reduce_fusion.1
  8.3 0.2 select_reduce_fusion.3
  8.5 0.1 select_subtract_fusion
  8.6 0.1 copy.35
  8.7 0.1 select_n.132.span_ref
  8.8 4.9 %select_reduce_fusion = s32[4,1024]{1,0:T(4,128)S(1)} fusion(s32[4,1024]{1,0:T(4,128)S(1)} %select_subtract_fusion, s32[4,1024]{1,0:T(4,128)S(1)} %select_reduce_fusion.1, pred[4,1024]{1,0:T(4,128)(4,1)S(1)} %get-tuple-element.126), kind=kLoop, calls=%fused_computation.1 | loop fusion | flops 16773120 | bytes 53248 | tf_op jit(solution)/shard_map/reduce_max | solution.py:131
  13.7 0.6 copy.44
  14.4 0.1 slice_add_fusion
  14.5 1.3 select_select_fusion
  15.7 0.0 copy-start
  15.7 30.7 %gather_rows.1 = bf16[4096,2048]{1,0:T(8,128)(2,1)} custom-call(s32[8]{0:T(128)S(1)} %select_n.132.span_ref, s32[4096]{0:T(1024)S(1)} %bitcast.28, s32[4096,1]{1,0:T(8,128)S(1)} %bitcast.27, bf16[8000,8,2048]{2,1,0:T(8,128)(2,1)} %bitcast.13.table_ref), custom_call_target="tpu_custom_call" | custom-call | flops 17179869184 | bytes 67108864 | tf_op jit(solution)/shard_map/gather_rows/pallas_call | solution.py:84
  46.5 0.0 copy-done
  46.5 0.6 broadcast_in_dim.86
  47.1 0.0 collective-permute-done
  47.1 0.6 maximum_reduce_fusion
  48.3 322.9 %conditional.1 = (bf16[1024,2048]{1,0:T(8,128)(2,1)}) conditional(s32[]{:T(128)} %convert_element_type.9, (bf16[1,2048]{1,0:T(2,128)(2,1)}, s32[2,1024,1]{1,0,2:T(2,128)S(1)}, s32[2,1024,1]{1,0,2:T(2,128)S(1)}, s32[2,1024,1]{2,1,0:T(8,128)}, bf16[4096,2048]{1,0:T(8,128)(2,1)}, /*index=5*/bf16[2048,4096]{1,0:T(8,128)(2,1)}, ...), branch_computations={%region_5.7_spmd, %region_6.8_spmd} | conditional | flops 137438953472 | bytes 268479488 | solution.py:376
  48.5 2.0 slice.8.source_ref
  50.5 1.4 copy.40.other_ref
  51.9 1.4 copy.39.ours_ref
  53.3 317.9 %mlp_block.3 = (bf16[1024,2048]{1,0:T(8,128)(2,1)}, bf16[2048,4096]{1,0:T(8,128)(2,1)}, bf16[4096,2048]{1,0:T(8,128)(2,1)}, f32[1024,2048]{1,0:T(8,128)}) custom-call(bf16[1,2048]{1,0:T(2,128)(2,1)} %get-tuple-element.45.gain_ref, s32[2,1024,1]{2,1,0:T(8,128)} %copy.39.ours_ref, s32[2,1024,1]{2,1,0:T(8,128)} %copy.40.other_ref, ...), custom_call_target="tpu_custom_call" | custom-call | flops 137438953472 | bytes 268435456 | tf_op jit(solution)/shard_map/cond/branch_1_fun/mlp_block/pallas_call | solution.py:335
  371.2 4.8 %copy.50 = bf16[1024,2048]{1,0:T(8,128)(2,1)} copy(bf16[1024,2048]{1,0:T(8,128)(2,1)} %get-tuple-element.53) | data formatting | bytes 8388608
  (15 shorter events, 0.2 us)
Async XLA Ops:
  4.6 42.5 %collective-permute-start = (s32[8,128]{1,0:T(8,128)S(1)}, s32[8,128]{1,0:T(8,128)S(1)}, u32[]{:S(2)}, u32[]{:S(2)}) collective-permute-start(s32[8,128]{1,0:T(8,128)S(1)} %broadcast_in_dim.85), channel_id=1, source_target_pairs={{0,4},{4,0},{1,5},{5,1},{2,6},{6,2},{3,7},{7,3}} | collective-permute-start | bytes 12296 | tf_op jit(solution)/shard_map/ppermute | solution.py:374
  15.7 30.8 %copy-start = (bf16[2048]{0:T(1024)(128)(2,1)S(1)}, bf16[2048]{0:T(1024)(128)(2,1)}, u32[]{:S(2)}) copy-start(bf16[2048]{0:T(1024)(128)(2,1)} %param.11) | copy-start | bytes 12292

commit v3 on v2

v3 whole, which is shorter than its diff:
```python
import functools

import jax
import jax.numpy as jnp
from jax import lax
from jax.experimental import pallas as pl
from jax.experimental.pallas import tpu as pltpu
from jax.sharding import PartitionSpec as P

RMS_EPS = 1e-6
TILE = 32
SLOTS = 6
PARTS = 4
PIECE = 128
CHUNK = 512
WIDTH = 512
PACKED = 704
MESH = pl.DeviceIdType.MESH


def ones_where(cond):
    return jnp.where(cond, 1.0, 0.0).astype(jnp.bfloat16)


def exact_dot(lhs, rhs):
    return jnp.dot(lhs.astype(jnp.bfloat16), rhs.astype(jnp.bfloat16), preferred_element_type=jnp.float32)


def gather_kernel(
    shard_rows, tokens_ref, table_ref, out_ref, place_ref, counts_ref,
    meta, meta_smem, picks, slabs, rows, steps, meta_sem, slab_sem, row_sem,
):
    me = lax.axis_index("tp")
    chip, core = lax.div(me, 2), lax.rem(me, 2)
    partner, other = me + 1 - 2 * core, lax.rem(me + 2, 4)
    other_partner = other + 1 - 2 * core
    blocks = [other_partner, partner, other, me]
    groups = meta.shape[0] // 3
    per = groups // 4

    ids = jnp.concatenate([tokens_ref[pl.ds(pl.multiple_of(b * per, per), per), :] for b in blocks], axis=0)
    owner = sum((ids >= q * shard_rows).astype(jnp.int32) for q in (1, 2, 3))
    mask = jnp.concatenate([jnp.where(owner == q, 1.0, 0.0) for q in range(4)], axis=0).astype(jnp.bfloat16)
    r = lax.broadcasted_iota(jnp.int32, (128, 128), 0)
    c = lax.broadcasted_iota(jnp.int32, (128, 128), 1)
    same = lax.div(r, per) == lax.div(c, per)
    ones = jnp.ones((128, 128), jnp.bfloat16)
    rank = exact_dot(mask, ones_where(r <= c)) + exact_dot(exact_dot(ones_where(same & (c < r)), mask), ones)
    total = exact_dot(exact_dot(ones_where(same), mask), ones)
    rank = [rank[q * groups:(q + 1) * groups] for q in range(4)]
    total = [total[q * groups:(q + 1) * groups] for q in range(4)]
    place = jnp.where(owner == 0, rank[0], jnp.where(
        owner == 1, rank[1] + total[0], jnp.where(owner == 2, rank[2], rank[3] + total[2])
    )).astype(jnp.int32) - 1
    ours = lax.shift_right_logical(owner, 1) == chip
    place_ref[0] = jnp.where(ours, place, -1)[groups // 2:].astype(jnp.float32)
    place_ref[1] = jnp.where(ours, -1, place)[groups // 2:].astype(jnp.float32)
    meta[pl.ds(groups, groups), :] = jnp.where(chip == 0, total[0], total[2]).astype(jnp.int32)
    meta[pl.ds(2 * groups, groups), :] = jnp.where(chip == 0, total[1], total[3]).astype(jnp.int32)

    local = jnp.where(owner == me, ids - me * shard_rows, 0)
    mine = owner == me
    high, low = lax.shift_right_logical(local, 8).astype(jnp.float32), (local & 255).astype(jnp.float32)
    place_group = lax.shift_right_logical(place, 7)
    eye = ones_where(r == c)
    dims = (((1,), (1,)), ((), ()))
    lane_of = lax.dot_general(
        eye, (place & 127).astype(jnp.float32).astype(jnp.bfloat16), dims, preferred_element_type=jnp.float32
    ).astype(jnp.int32)
    group_row = lax.broadcasted_iota(jnp.int32, (per, 128), 0)
    found = []
    for b in range(4):
        acc = jnp.zeros((2 * per, 128), jnp.float32)
        for g in range(b * per, (b + 1) * per):
            hit = (place_group[g:g + 1] == group_row) & mine[g:g + 1]
            lhs = jnp.concatenate([jnp.where(hit, high[g:g + 1], 0.0), jnp.where(hit, low[g:g + 1], 0.0)], axis=0)
            acc = acc + exact_dot(lhs, ones_where(lane_of[:, g:g + 1] == c))
        found.append(acc[:per] * 256.0 + acc[per:])
    found = jnp.concatenate(found, axis=0).astype(jnp.int32)
    meta[pl.ds(0, groups), :] = lax.shift_right_logical(found, 3)
    row_of = lax.dot_general(
        eye, (found & 7).astype(jnp.float32).astype(jnp.bfloat16), dims, preferred_element_type=jnp.float32
    ).astype(jnp.int32)
    for g in range(groups):
        picks[pl.ds(g * 128, 128), :] = jnp.broadcast_to(row_of[:, g:g + 1], (128, 128))

    to_smem = pltpu.make_async_copy(meta, meta_smem, meta_sem)
    to_smem.start()
    to_smem.wait()

    tiles = per * 128 // TILE
    n_steps = 0
    for b in range(4):
        count0, count1 = meta_smem[groups + b * per, 0], meta_smem[2 * groups + b * per, 0]
        if b >= 2:
            counts_ref[2 * (b - 2)] = count0
            counts_ref[2 * (b - 2) + 1] = count0 + count1
        start = jnp.where(core == 0, 0, count0)
        end = jnp.where(core == 0, count0, count0 + count1)
        first = lax.div(start, TILE)
        last = jnp.where(end > start, lax.div(end + TILE - 1, TILE), first)

        def note(t, _, b=b, first=first, n_steps=n_steps):
            steps[n_steps + t - first] = b * tiles + t
            return 0

        lax.fori_loop(first, last, note, 0)
        n_steps = n_steps + last - first

    def fetch(step):
        slot = lax.rem(step, SLOTS)
        tile = steps[step]
        group, lane = lax.div(tile, 128 // TILE), lax.rem(tile, 128 // TILE) * TILE
        for j in range(TILE):
            pltpu.make_async_copy(
                table_ref.at[meta_smem[group, lane + j]], slabs.at[slot, pl.ds(8 * j, 8), :], slab_sem.at[slot]
            ).start()

    for step in range(SLOTS - 1):
        @pl.when(step < n_steps)
        def _(step=step):
            fetch(step)

    def out_copy(step):
        slot = lax.rem(step, 2)
        return pltpu.make_async_copy(
            rows.at[slot], out_ref.at[pl.ds(steps[step] * TILE, TILE), :], row_sem.at[slot]
        )

    def work(step, _):
        @pl.when(step + SLOTS - 1 < n_steps)
        def _():
            fetch(step + SLOTS - 1)

        slot = lax.rem(step, SLOTS)
        pltpu.make_async_copy(slabs.at[slot], slabs.at[slot], slab_sem.at[slot]).wait()
        base = pl.multiple_of(steps[step] * TILE, TILE)
        pick = picks[pl.ds(base, TILE), :]
        col = lax.broadcasted_iota(jnp.int32, (TILE, 8 * TILE), 1)
        want = jnp.concatenate([pick] * (8 * TILE // 128), axis=1) + 8 * lax.broadcasted_iota(
            jnp.int32, (TILE, 8 * TILE), 0
        )

        @pl.when(step >= 2)
        def _():
            out_copy(step - 2).wait()

        rows[lax.rem(step, 2)] = exact_dot(ones_where(col == want), slabs[slot]).astype(jnp.bfloat16)
        out_copy(step).start()
        return 0

    lax.fori_loop(0, n_steps, work, 0)
    for back in (2, 1):
        @pl.when(n_steps >= back)
        def _(back=back):
            out_copy(n_steps - back).wait()


def gather_rows(token_ids, table_shard):
    n_ids, (shard_rows, dim) = token_ids.shape[0], table_shard.shape
    groups = n_ids // 128
    smem, vmem = pl.BlockSpec(memory_space=pltpu.SMEM), pl.BlockSpec(memory_space=pltpu.VMEM)
    return pl.pallas_call(
        functools.partial(gather_kernel, shard_rows),
        out_shape=[
            jax.ShapeDtypeStruct((n_ids, dim), jnp.bfloat16),
            jax.ShapeDtypeStruct((2, groups // 2, 128), jnp.float32),
            jax.ShapeDtypeStruct((4,), jnp.int32),
        ],
        in_specs=[vmem, pl.BlockSpec(memory_space=pl.ANY)],
        out_specs=[pl.BlockSpec(memory_space=pl.ANY), vmem, smem],
        scratch_shapes=[
            pltpu.VMEM((3 * groups, 128), jnp.int32),
            pltpu.SMEM((3 * groups, 128), jnp.int32),
            pltpu.VMEM((n_ids, 128), jnp.int32),
            pltpu.VMEM((SLOTS, 8 * TILE, dim), jnp.bfloat16),
            pltpu.VMEM((2, TILE, dim), jnp.bfloat16),
            pltpu.SMEM((n_ids // TILE,), jnp.int32),
            pltpu.SemaphoreType.DMA,
            pltpu.SemaphoreType.DMA((SLOTS,)),
            pltpu.SemaphoreType.DMA((2,)),
        ],
        compiler_params=pltpu.CompilerParams(vmem_limit_bytes=40 << 20),
        cost_estimate=pl.CostEstimate(flops=1 << 34, bytes_accessed=1 << 26, transcendentals=0),
        name="gather_rows",
    )(token_ids.reshape(groups, 128), table_shard.reshape(-1, 8, dim))


def block_kernel(
    cap, stride, gain_ref, place_ref, counts_ref, rows_ref, w1_ref, w2_ref,
    out_ref, w1p_ref, w2p_ref, sums_ref,
    inbox, ours_rows, normed, kept, acc, w1_buf, w2_buf, sum_buf, out_buf,
    pair_send, pair_recv, load_sem, w_send, w_recv, ready, x_send, x_recv, w_sem, s_send, s_recv, r_sem, o_sem,
):
    me, dp = lax.axis_index("tp"), lax.axis_index("dp")
    core = lax.rem(me, 2)
    partner = me + 1 - 2 * core
    other = lax.rem(me + 2, 4)
    dim = gain_ref.shape[1]
    n_tok = out_ref.shape[0]
    width = w1_ref.shape[1]
    w_steps = width // WIDTH
    n_chunks = n_tok // CHUNK
    n_pieces = n_tok // PIECE

    barrier = pltpu.get_barrier_semaphore()
    for peer in (partner, other):
        pl.semaphore_signal(barrier, inc=1, device_id=(dp, peer), device_id_type=MESH)
    pl.semaphore_wait(barrier, 2)

    def remote(src, dst, send, recv, peer):
        return pltpu.make_async_remote_copy(
            src_ref=src, dst_ref=dst, send_sem=send, recv_sem=recv, device_id=(dp, peer), device_id_type=MESH
        )

    part = cap // PARTS
    parts = [(p, q) for p in range(2) for q in range(PARTS)]

    def pair(p, q):
        src = pl.ds((1 - p) * stride + q * part, part)
        return remote(
            rows_ref.at[src, :], inbox.at[p, pl.ds(q * part, part), :], pair_send.at[p, q], pair_recv.at[p, q], partner
        )

    def load(p, q):
        src = pl.ds((3 - p) * stride + q * part, part)
        return pltpu.make_async_copy(
            rows_ref.at[src, :], ours_rows.at[1 - p, pl.ds(q * part, part), :], load_sem.at[p, q]
        )

    def cross(p, q):
        span = pl.ds(q * part, part)
        return remote(
            ours_rows.at[1 - p, span, :], inbox.at[p, span, :], x_send.at[p, q], x_recv.at[p, q], other
        )

    weights = [
        remote(w1_ref, w1p_ref, w_send.at[0], w_recv.at[0], partner),
        remote(w2_ref, w2p_ref, w_send.at[1], w_recv.at[1], partner),
    ]
    for p, q in parts:
        pair(p, q).start()
        load(p, q).start()
    for copy in weights:
        copy.start()

    def fetch_weights(step, slot, start):
        @pl.when(step < w_steps)
        def _():
            cols = pl.ds(pl.multiple_of(step * WIDTH, WIDTH), WIDTH)
            start(pltpu.make_async_copy(w1_ref.at[:, cols], w1_buf.at[slot], w_sem.at[0, slot]))
            start(pltpu.make_async_copy(w2_ref.at[cols, :], w2_buf.at[slot], w_sem.at[1, slot]))

        @pl.when(step >= w_steps)
        def _():
            cols = pl.ds(pl.multiple_of((step - w_steps) * WIDTH, WIDTH), WIDTH)
            start(pltpu.make_async_copy(w1p_ref.at[:, cols], w1_buf.at[slot], w_sem.at[0, slot]))
            start(pltpu.make_async_copy(w2p_ref.at[cols, :], w2_buf.at[slot], w_sem.at[1, slot]))

    fetch_weights(0, 0, lambda copy: copy.start())

    for p, q in parts:
        b = 1 - p
        load(p, q).wait()
        pair(p, q).wait_recv()
        core0_end, chip_end = counts_ref[2 * b], counts_ref[2 * b + 1]

        @pl.loop(0, part // 16)
        def _(t, p=p, q=q, b=b, core0_end=core0_end, chip_end=chip_end):
            base = pl.multiple_of(q * part + t * 16, 16)
            span = pl.ds(base, 16)
            pos = base + lax.broadcasted_iota(jnp.int32, (16, dim), 0)
            mine = ours_rows[b, span, :].astype(jnp.float32)
            theirs = inbox[p, span, :].astype(jnp.float32)
            from_core = jnp.where(pos < core0_end, 0, 1)
            merged = jnp.where(from_core == core, mine, theirs)
            ours_rows[b, span, :] = jnp.where(pos < chip_end, merged, 0.0).astype(jnp.bfloat16)

        pl.semaphore_signal(ready.at[p, q], inc=1, device_id=(dp, other), device_id_type=MESH)
        pl.semaphore_wait(ready.at[p, q], 1)
        cross(p, q).start()

    gain = gain_ref[...].astype(jnp.float32)

    sums_land = sum_buf if cap < n_tok else sums_ref

    def send_sums(piece):
        span = pl.ds(pl.multiple_of(piece * PIECE, PIECE), PIECE)
        return remote(acc.at[span, :], sums_land.at[span, :], s_send.at[piece], s_recv.at[piece], other)

    @pl.loop(0, 2)
    def _(b):
        for q in range(PARTS):
            span = pl.ds(q * part, part)
            remote(
                ours_rows.at[1 - b, span, :], inbox.at[b, span, :], x_send.at[b, q], x_recv.at[b, q], other
            ).wait_recv()

        @pl.loop(0, n_tok // 256)
        def _(t):
            span = pl.ds(pl.multiple_of(t * 256, 256), 256)
            slot = lax.broadcasted_iota(jnp.int32, (128, cap), 1).astype(jnp.float32)
            diagonal = lax.broadcasted_iota(jnp.int32, (128, 128), 0) == lax.broadcasted_iota(
                jnp.int32, (128, 128), 1
            )

            def pick_from(side):
                picks = []
                for g in range(2):
                    row = place_ref[side, pl.ds(b * (n_tok // 128) + 2 * t + g, 1), :]
                    column = jnp.sum(jnp.where(diagonal, row, 0.0), axis=1, keepdims=True)
                    picks.append(ones_where(slot == column))
                return jnp.concatenate(picks, axis=0)

            pick_ours, pick_other = pick_from(0), pick_from(1)
            rows = jnp.dot(pick_ours, ours_rows[b], preferred_element_type=jnp.float32) + jnp.dot(
                pick_other, inbox[b], preferred_element_type=jnp.float32
            )
            kept[span, :] = rows.astype(jnp.bfloat16)
            inv_rms = lax.rsqrt(jnp.mean(rows * rows, axis=-1, keepdims=True) + RMS_EPS)
            normed[span, :] = (rows * inv_rms * gain).astype(jnp.bfloat16)

        @pl.loop(0, n_chunks)
        def _(chunk):
            tok = pl.ds(pl.multiple_of(chunk * CHUNK, CHUNK), CHUNK)
            out_rows = pl.ds(pl.multiple_of(b * n_tok + chunk * CHUNK, CHUNK), CHUNK)
            acc[out_rows, :] = jnp.zeros((CHUNK, dim), jnp.float32)

            @pl.loop(0, 2 * w_steps)
            def _(w):
                step = (b * n_chunks + chunk) * 2 * w_steps + w
                slot = lax.rem(step, 2)
                fetch_weights(w, slot, lambda copy: copy.wait())

                @pl.when(step == w_steps - 1)
                def _():
                    for copy in weights:
                        copy.wait_recv()

                @pl.when(step + 1 < 2 * n_chunks * 2 * w_steps)
                def _():
                    fetch_weights(lax.rem(step + 1, 2 * w_steps), 1 - slot, lambda copy: copy.start())

                parts = []
                for half in range(2):
                    cols = pl.ds(half * (WIDTH // 2), WIDTH // 2)
                    z = jnp.dot(normed[tok, :], w1_buf[slot, :, cols], preferred_element_type=jnp.float32)
                    z = z.astype(jnp.bfloat16).astype(jnp.float32)
                    inner = 0.7978845608028654 * (z + 0.044715 * (z * z * z))
                    parts.append((0.5 * z * (1.0 + jnp.tanh(inner))).astype(jnp.bfloat16))
                hidden = jnp.concatenate(parts, axis=1)
                for half in range(2):
                    cols = pl.ds(half * (dim // 2), dim // 2)
                    acc[out_rows, cols] += jnp.dot(
                        hidden, w2_buf[slot, :, cols], preferred_element_type=jnp.float32
                    )

            @pl.when(b == 0)
            def _():
                for q in range(CHUNK // PIECE):
                    send_sums(chunk * (CHUNK // PIECE) + q).start()

    sums_in_vmem = cap < n_tok

    def take_sums(piece, slot):
        span = pl.ds(pl.multiple_of(piece * PIECE, PIECE), PIECE)
        return pltpu.make_async_copy(sums_ref.at[span, :], sum_buf.at[slot], r_sem.at[slot])

    def put_out(piece, slot):
        span = pl.ds(pl.multiple_of(piece * PIECE, PIECE), PIECE)
        return pltpu.make_async_copy(out_buf.at[slot], out_ref.at[span, :], o_sem.at[slot])

    @pl.loop(0, n_pieces)
    def _(piece):
        slot = lax.rem(piece, 2)
        send_sums(piece).wait_recv()
        if not sums_in_vmem:
            take = take_sums(piece, slot)
            take.start()
            take.wait()

        @pl.when(piece >= 2)
        def _():
            put_out(piece - 2, slot).wait()

        span = pl.ds(pl.multiple_of(piece * PIECE, PIECE), PIECE)
        own = pl.ds(pl.multiple_of(n_tok + piece * PIECE, PIECE), PIECE)
        total = acc[own, :] + (sums_land[span, :] if sums_in_vmem else sum_buf[slot])
        out_buf[slot] = (kept[span, :].astype(jnp.float32) + total).astype(jnp.bfloat16)
        put_out(piece, slot).start()

    put_out(n_pieces - 2, lax.rem(n_pieces - 2, 2)).wait()
    put_out(n_pieces - 1, lax.rem(n_pieces - 1, 2)).wait()

    for copy in [pair(*at) for at in parts] + weights + [cross(*at) for at in parts]:
        copy.wait_send()

    @pl.loop(0, n_pieces)
    def _(piece):
        send_sums(piece).wait_send()


def mlp_block(cap, collective_id, gain, place, counts, rows, w_in, w_out):
    n_tok = rows.shape[0] // 4
    dim, width = w_in.shape
    any_spec, vmem = pl.BlockSpec(memory_space=pl.ANY), pl.BlockSpec(memory_space=pltpu.VMEM)
    smem = pl.BlockSpec(memory_space=pltpu.SMEM)
    dma = pltpu.SemaphoreType.DMA
    n_pieces = n_tok // PIECE
    flops = 2 * (2 * n_tok) * dim * (2 * width) * 2
    return pl.pallas_call(
        functools.partial(block_kernel, cap, n_tok),
        out_shape=[
            jax.ShapeDtypeStruct((n_tok, dim), jnp.bfloat16),
            jax.ShapeDtypeStruct(w_in.shape, w_in.dtype),
            jax.ShapeDtypeStruct(w_out.shape, w_out.dtype),
            jax.ShapeDtypeStruct((n_tok if cap == n_tok else 8, dim), jnp.float32),
        ],
        in_specs=[vmem, vmem, smem, any_spec, any_spec, any_spec],
        out_specs=[any_spec] * 4,
        scratch_shapes=[
            pltpu.VMEM((2, cap, dim), jnp.bfloat16),
            pltpu.VMEM((2, cap, dim), jnp.bfloat16),
            pltpu.VMEM((n_tok, dim), jnp.bfloat16),
            pltpu.VMEM((n_tok, dim), jnp.bfloat16),
            pltpu.VMEM((2 * n_tok, dim), jnp.float32),
            pltpu.VMEM((2, dim, WIDTH), jnp.bfloat16),
            pltpu.VMEM((2, WIDTH, dim), jnp.bfloat16),
            pltpu.VMEM((2, PIECE, dim) if cap == n_tok else (n_tok, dim), jnp.float32),
            pltpu.VMEM((2, PIECE, dim), jnp.bfloat16),
            dma((2, PARTS)), dma((2, PARTS)), dma((2, PARTS)), dma((2,)), dma((2,)),
            pltpu.SemaphoreType.REGULAR((2, PARTS)),
            dma((2, PARTS)), dma((2, PARTS)), dma((2, 2)), dma((n_pieces,)), dma((n_pieces,)), dma((2,)), dma((2,)),
        ],
        compiler_params=pltpu.CompilerParams(
            collective_id=collective_id, has_side_effects=True, vmem_limit_bytes=67043328
        ),
        cost_estimate=pl.CostEstimate(flops=flops, bytes_accessed=1 << 28, transcendentals=0),
        name="mlp_block",
    )(gain, place, counts, rows, w_in, w_out)[0]


def copy_kernel(src_ref, dst_ref, buf, in_sem, out_sem):
    n = buf.shape[0]
    rows = buf.shape[1]
    ins = [pltpu.make_async_copy(src_ref.at[pl.ds(i * rows, rows), :], buf.at[i], in_sem.at[i]) for i in range(n)]
    outs = [pltpu.make_async_copy(buf.at[i], dst_ref.at[pl.ds(i * rows, rows), :], out_sem.at[i]) for i in range(n)]
    for copy in ins:
        copy.start()
    for i in range(n):
        ins[i].wait()
        outs[i].start()
    for copy in outs:
        copy.wait()


def copy_out(x):
    n = 8
    return pl.pallas_call(
        copy_kernel,
        out_shape=jax.ShapeDtypeStruct(x.shape, x.dtype),
        in_specs=[pl.BlockSpec(memory_space=pl.ANY)],
        out_specs=pl.BlockSpec(memory_space=pl.ANY),
        scratch_shapes=[
            pltpu.VMEM((n, x.shape[0] // n, x.shape[1]), x.dtype),
            pltpu.SemaphoreType.DMA((n,)),
            pltpu.SemaphoreType.DMA((n,)),
        ],
        compiler_params=pltpu.CompilerParams(vmem_limit_bytes=62 << 20),
        name="copy_out",
    )(x)


def solution(mesh):
    swap = [(0, 1), (1, 0)]

    def device_step(token_ids, table_shard, norm_gain, w_in_shard, w_out_shard):
        n_tok = token_ids.shape[0] // 4
        on_chip1 = jnp.sum((token_ids.reshape(4, n_tok) >= 2 * table_shard.shape[0]).astype(jnp.int32), axis=1)
        most = jnp.full((8, 128), jnp.max(jnp.maximum(on_chip1, n_tok - on_chip1)), jnp.int32)
        most = jnp.max(jnp.maximum(most, lax.ppermute(most, "dp", swap)))
        rows, place, counts = gather_rows(token_ids, table_shard)
        out = lax.cond(
            most <= PACKED,
            functools.partial(mlp_block, PACKED, 0),
            functools.partial(mlp_block, n_tok, 1),
            norm_gain[None, :], place, counts, rows, w_in_shard, w_out_shard,
        )
        return copy_out(out)

    return jax.shard_map(
        device_step,
        mesh=mesh,
        in_specs=(P("dp"), P("tp", None), P(), P(None, "tp"), P("tp", None)),
        out_specs=P(("dp", "tp"), None),
        check_vma=False,
    )
```

time: 377 us -> 358 us (0.950)
  local copies, waits for them, and re-layouts: 12.8 us -> 1.89 us
  other arithmetic: 8.66 us -> 2.75 us
    pallas_call x1, Pallas kernels: 318 us -> 311 us  [mlp_block(): pl.pallas_call(functools.partial(block_kernel, cap, n_tok), out_shape=[ja...]
    pallas_call x1 -> x2, Pallas kernels: 30.7 us -> 36.7 us  [the longest x1 33.2 us: gather_rows(): pl.pallas_call(functools.partial(gather_kernel, shard_rows), out_shape=[j...]
    unnamed x7 -> x4, local copies, waits for them, and re-layouts: 5.57 us -> 0.72 us
    reduce_max x1, other arithmetic: 4.93 us -> 0.63 us  [device_step(): jnp.max(jnp.maximum(on_chip1, n_tok - on_chip1))]
  transfers between devices with their start and end apart: 1 -> 1, of which waited for: 0 -> 0; matrix products, arithmetic and copies ran while one was open for 2% -> 0% of each run, Pallas kernels for 8% -> 9%
where the time goes in v3:
time: 358 us; the launch traced here: 357 us
  Pallas kernels  348 us (97%)
    pallas_call x1, Pallas kernels, mlp_block(): pl.pallas_call(functools.partial(block_kernel, cap, n_tok), out_shape=[ja...  311 us
    pallas_call x1, Pallas kernels, gather_rows(): pl.pallas_call(functools.partial(gather_kernel, shard_rows), out_shape=[j...  33.2 us
  transfers between devices with their start and end apart: 1, of which 0 were waited for; matrix products, arithmetic and copies ran while one was open for 0% of the time, Pallas kernels for 9%

profile of v3, /device:TPU:0, one launch (start us, length us, event | category | flops | bytes accessed | tf_op | source)
XLA Modules:
  0.0 357.0 jit_solution(14488764178504591067)
XLA Ops:
  0.0 0.7 compare_convert_fusion
  0.7 0.1 reduce_sum.9
  0.9 0.6 fusion
  1.5 0.6 broadcast_in_dim.6
  2.1 3.4 collective-permute-start
  5.5 0.0 copy-start
  5.5 0.7 copy-done
  6.2 0.0 copy-start.1
  6.2 33.2 %gather_rows.1 = (bf16[4096,2048]{1,0:T(8,128)(2,1)}, f32[2,16,128]{2,1,0:T(8,128)}, s32[4]{0:T(128)}) custom-call(s32[32,128]{1,0:T(8,128)S(1)} %bitcast.2, bf16[8000,8,2048]{2,1,0:T(8,128)(2,1)} %bitcast.1.table_ref), custom_call_target="tpu_custom_call" | custom-call | flops 17179869184 | bytes 67108864 | tf_op jit(solution)/shard_map/gather_rows/pallas_call | solution.py:163
  39.3 0.0 copy-done.1
  39.3 0.6 broadcast_in_dim.7
  39.9 0.0 collective-permute-done
  39.9 1.3 maximum_reduce_fusion
  41.9 311.4 %conditional.1 = (bf16[1024,2048]{1,0:T(8,128)(2,1)}) conditional(s32[]{:T(128)} %convert_element_type.11, (bf16[1,2048]{1,0:T(2,128)(2,1)}, f32[2,16,128]{2,1,0:T(8,128)}, s32[4]{0:T(128)}, bf16[4096,2048]{1,0:T(8,128)(2,1)}, bf16[2048,4096]{1,0:T(8,128)(2,1)}, /*index=5*/bf16[4096,2048]{1,0:T(8,128)(2,1)}) %tuple.11, (bf16[1,2048]{1,0:T(2,128)(2,1)}, ...), branch_computations={%region_3.0_spmd, %region_4.0_spmd} | conditional | flops 137438953472 | bytes 268435456 | solution.py:483
  42.1 311.2 %mlp_block.3 = (bf16[1024,2048]{1,0:T(8,128)(2,1)}, bf16[2048,4096]{1,0:T(8,128)(2,1)}, bf16[4096,2048]{1,0:T(8,128)(2,1)}, f32[8,2048]{1,0:T(8,128)}) custom-call(bf16[1,2048]{1,0:T(2,128)(2,1)} %get-tuple-element.39.gain_ref, f32[2,16,128]{2,1,0:T(8,128)} %get-tuple-element.40.place_ref, s32[4]{0:T(128)} %get-tuple-element.41.counts_ref, ...), custom_call_target="tpu_custom_call" | custom-call | flops 137438953472 | bytes 268435456 | tf_op jit(solution)/shard_map/cond/branch_1_fun/mlp_block/pallas_call | solution.py:411
  353.3 3.6 %copy_out.1 = bf16[1024,2048]{1,0:T(8,128)(2,1)} custom-call(bf16[1024,2048]{1,0:T(8,128)(2,1)} %get-tuple-element.52.src_ref), custom_call_target="tpu_custom_call" | custom-call | tf_op jit(solution)/shard_map/copy_out/pallas_call | solution.py:459
  (1 shorter events, 0.0 us)
Async XLA Ops:
  2.1 37.9 %collective-permute-start = (s32[8,128]{1,0:T(8,128)S(1)}, s32[8,128]{1,0:T(8,128)S(1)}, u32[]{:S(2)}, u32[]{:S(2)}) collective-permute-start(s32[8,128]{1,0:T(8,128)S(1)} %broadcast_in_dim.6), channel_id=1, source_target_pairs={{0,4},{4,0},{1,5},{5,1},{2,6},{6,2},{3,7},{7,3}} | collective-permute-start | bytes 12296 | tf_op jit(solution)/shard_map/ppermute | solution.py:481
  5.5 0.7 copy-start
  6.2 33.2 %copy-start.1 = (bf16[2048]{0:T(1024)(128)(2,1)S(1)}, bf16[2048]{0:T(1024)(128)(2,1)}, u32[]{:S(2)}) copy-start(bf16[2048]{0:T(1024)(128)(2,1)} %param.9) | copy-start | bytes 12292

commit v4 on v3

v4 whole, which is shorter than its diff:
```python
import functools

import jax
import jax.numpy as jnp
from jax import lax
from jax.experimental import pallas as pl
from jax.experimental.pallas import tpu as pltpu
from jax.sharding import PartitionSpec as P

RMS_EPS = 1e-6
TILE = 64
PICK = 32
SLOTS = 4
EARLY = 128
GROUPS = 16
PIECE = 128
CHUNK = 512
WIDTH = 512
PACKED = (672, 704)
MESH = pl.DeviceIdType.MESH


def ones_where(cond):
    return jnp.where(cond, 1.0, 0.0).astype(jnp.bfloat16)


def exact_dot(lhs, rhs):
    return jnp.dot(lhs.astype(jnp.bfloat16), rhs.astype(jnp.bfloat16), preferred_element_type=jnp.float32)


def fetch_slabs(table_ref, slab_ids, group, lane, slabs, slot, sem):
    for j in range(TILE):
        pltpu.make_async_copy(
            table_ref.at[slab_ids(group, lane + j)], slabs.at[slot, pl.ds(8 * j, 8), :], sem.at[slot]
        ).start()


def pick_rows(picks, base, slabs, slot, sem, rows, row_slot):
    pltpu.make_async_copy(slabs.at[slot], slabs.at[slot], sem.at[slot]).wait()
    col = lax.broadcasted_iota(jnp.int32, (PICK, 8 * PICK), 1)
    first_col = 8 * lax.broadcasted_iota(jnp.int32, (PICK, 8 * PICK), 0)
    for part in range(TILE // PICK):
        pick = picks[pl.ds(base + part * PICK, PICK), :]
        want = jnp.concatenate([pick] * (8 * PICK // 128), axis=1) + first_col
        rows[row_slot, pl.ds(part * PICK, PICK), :] = exact_dot(
            ones_where(col == want), slabs[slot, pl.ds(part * 8 * PICK, 8 * PICK), :]
        ).astype(jnp.bfloat16)


def to_column(eye, values):
    return lax.dot_general(
        eye, values.astype(jnp.float32).astype(jnp.bfloat16), (((1,), (1,)), ((), ())),
        preferred_element_type=jnp.float32,
    ).astype(jnp.int32)


def early_kernel(
    shard_rows, tokens_ref, table_ref, part_ref, mine_ref, found_ref, place_ref, counts_ref, rests_ref,
    slab_no, slab_no_smem, picks, slabs, rows, meta_sem, slab_sem, row_sem,
):
    me = lax.axis_index("tp")
    chip, core = lax.div(me, 2), lax.rem(me, 2)
    partner, other = me + 1 - 2 * core, lax.rem(me + 2, 4)
    other_partner = other + 1 - 2 * core
    blocks = [other_partner, partner, other, me]
    groups = tokens_ref.shape[0]
    per = groups // 4

    ids = jnp.concatenate([tokens_ref[pl.ds(pl.multiple_of(b * per, per), per), :] for b in blocks], axis=0)
    owner = sum((ids >= q * shard_rows).astype(jnp.int32) for q in (1, 2, 3))
    mask = jnp.concatenate([jnp.where(owner == q, 1.0, 0.0) for q in range(4)], axis=0).astype(jnp.bfloat16)
    r = lax.broadcasted_iota(jnp.int32, (128, 128), 0)
    c = lax.broadcasted_iota(jnp.int32, (128, 128), 1)
    same = lax.div(r, per) == lax.div(c, per)
    ones = jnp.ones((128, 128), jnp.bfloat16)
    rank = exact_dot(mask, ones_where(r <= c)) + exact_dot(exact_dot(ones_where(same & (c < r)), mask), ones)
    total = exact_dot(exact_dot(ones_where(same), mask), ones)
    rank = [rank[q * groups:(q + 1) * groups] - 1.0 for q in range(4)]
    rest = [jnp.maximum(total[q * groups:(q + 1) * groups] - EARLY, 0.0) for q in range(4)]

    def placed(q):
        late = EARLY + (rest[q - 1] if q % 2 else 0.0)
        return rank[q] + jnp.where(rank[q] < EARLY, float(EARLY * (q % 2)), late)

    place = jnp.where(owner == 0, placed(0), jnp.where(
        owner == 1, placed(1), jnp.where(owner == 2, placed(2), placed(3))
    )).astype(jnp.int32)
    ours = lax.shift_right_logical(owner, 1) == chip
    place_ref[0] = jnp.where(ours, place, -1)[groups // 2:].astype(jnp.float32)
    place_ref[1] = jnp.where(ours, -1, place)[groups // 2:].astype(jnp.float32)
    counts_ref[pl.ds(0, groups), :] = jnp.where(chip == 0, rest[0], rest[2]).astype(jnp.int32)
    counts_ref[pl.ds(groups, groups), :] = jnp.where(chip == 0, rest[1], rest[3]).astype(jnp.int32)

    for i in range(4):
        row = (i % 2) * groups + (2 + i // 2) * per
        rests_ref[pl.ds(i, 1), :] = counts_ref[pl.ds(row, 1), :]

    mine = owner == me
    local = jnp.where(mine, ids - me * shard_rows, 0)
    high, low = lax.shift_right_logical(local, 8).astype(jnp.float32), (local & 255).astype(jnp.float32)
    place_group = lax.shift_right_logical(place, 7)
    eye = ones_where(r == c)
    lane_of = to_column(eye, place & 127)
    group_row = lax.broadcasted_iota(jnp.int32, (GROUPS, 128), 0)
    for b in (1, 3, 0, 2):
        acc = jnp.zeros((2 * GROUPS, 128), jnp.float32)
        for g in range(b * per, (b + 1) * per):
            hit = (place_group[g:g + 1] == group_row) & mine[g:g + 1]
            lhs = jnp.concatenate([jnp.where(hit, high[g:g + 1], 0.0), jnp.where(hit, low[g:g + 1], 0.0)], axis=0)
            acc = acc + exact_dot(lhs, ones_where(lane_of[:, g:g + 1] == c))
        found_ref[pl.ds(b * GROUPS, GROUPS), :] = (acc[:GROUPS] * 256.0 + acc[GROUPS:]).astype(jnp.int32)

    early_groups = 2 * EARLY // 128
    for i, b in enumerate((1, 3)):
        found = found_ref[pl.ds(b * GROUPS, GROUPS), :]
        slab_no[pl.ds(i * GROUPS, GROUPS), :] = lax.shift_right_logical(found, 3)
        row_of = to_column(eye, found & 7)
        for g in range(early_groups):
            picks[pl.ds((i * early_groups + g) * 128, 128), :] = jnp.broadcast_to(row_of[:, g:g + 1], (128, 128))
    to_smem = pltpu.make_async_copy(slab_no, slab_no_smem, meta_sem)
    to_smem.start()
    to_smem.wait()

    n = EARLY // TILE
    for i in range(2):
        for t in range(n):
            at = core * EARLY + t * TILE
            fetch_slabs(
                table_ref, lambda group, lane: slab_no_smem[group, lane],
                i * GROUPS + lax.div(at, 128), lax.rem(at, 128), slabs, i * n + t, slab_sem,
            )
    outs = []
    for i in range(2):
        for t in range(n):
            step = i * n + t
            base = pl.multiple_of(i * early_groups * 128 + core * EARLY + t * TILE, TILE)
            pick_rows(picks, base, slabs, step, slab_sem, rows, step)
            target = (part_ref, mine_ref)[i]
            outs.append(pltpu.make_async_copy(rows.at[step], target.at[pl.ds(t * TILE, TILE), :], row_sem.at[step]))
            outs[-1].start()
    for copy in outs:
        copy.wait()


def early_rows(token_ids, table):
    n_ids, (slab_count, _, dim) = token_ids.shape[0], table.shape
    groups, steps = n_ids // 128, 2 * EARLY // TILE
    any_spec, vmem = pl.BlockSpec(memory_space=pl.ANY), pl.BlockSpec(memory_space=pltpu.VMEM)
    rows = jax.ShapeDtypeStruct((EARLY, dim), jnp.bfloat16)
    return pl.pallas_call(
        functools.partial(early_kernel, 8 * slab_count),
        out_shape=[
            rows, rows,
            jax.ShapeDtypeStruct((4 * GROUPS, 128), jnp.int32),
            jax.ShapeDtypeStruct((2, groups // 2, 128), jnp.float32),
            jax.ShapeDtypeStruct((2 * groups, 128), jnp.int32),
            jax.ShapeDtypeStruct((4, 128), jnp.int32),
        ],
        in_specs=[vmem, any_spec],
        out_specs=[any_spec, any_spec, vmem, vmem, vmem, vmem],
        scratch_shapes=[
            pltpu.VMEM((2 * GROUPS, 128), jnp.int32),
            pltpu.SMEM((2 * GROUPS, 128), jnp.int32),
            pltpu.VMEM((4 * EARLY, 128), jnp.int32),
            pltpu.VMEM((steps, 8 * TILE, dim), jnp.bfloat16),
            pltpu.VMEM((steps, TILE, dim), jnp.bfloat16),
            pltpu.SemaphoreType.DMA,
            pltpu.SemaphoreType.DMA((steps,)),
            pltpu.SemaphoreType.DMA((steps,)),
        ],
        compiler_params=pltpu.CompilerParams(vmem_limit_bytes=40 << 20),
        cost_estimate=pl.CostEstimate(flops=1 << 32, bytes_accessed=1 << 25, transcendentals=0),
        name="early_rows",
    )(token_ids.reshape(groups, 128), table)


def gather_kernel(found_ref, counts_ref, found_vmem, table_ref, out_ref, picks, slabs, rows, steps, slab_sem, row_sem):
    core = lax.rem(lax.axis_index("tp"), 2)
    half = counts_ref.shape[0] // 2
    eye = ones_where(
        lax.broadcasted_iota(jnp.int32, (128, 128), 0) == lax.broadcasted_iota(jnp.int32, (128, 128), 1)
    )
    row_of = to_column(eye, found_vmem[...] & 7)
    per_block = out_ref.shape[0] // 4
    for b in range(4):
        for g in range(per_block // 128):
            picks[pl.ds(b * per_block + g * 128, 128), :] = jnp.broadcast_to(
                row_of[:, b * GROUPS + g:b * GROUPS + g + 1], (128, 128)
            )

    tiles = per_block // TILE
    n_steps = 0
    for b in (1, 3, 0, 2):
        rest0, rest1 = counts_ref[b * (half // 4), 0], counts_ref[half + b * (half // 4), 0]
        start = jnp.where(core == 0, 2 * EARLY, 2 * EARLY + rest0)
        end = jnp.where(core == 0, 2 * EARLY + rest0, 2 * EARLY + rest0 + rest1)
        if b % 2 == 0:
            for t in range(EARLY // TILE):
                steps[n_steps + t] = b * tiles + core * (EARLY // TILE) + t
            n_steps = n_steps + EARLY // TILE
        first = lax.div(start, TILE)
        last = jnp.where(end > start, lax.div(end + TILE - 1, TILE), first)

        def note(t, _, b=b, first=first, n_steps=n_steps):
            steps[n_steps + t - first] = b * tiles + t
            return 0

        lax.fori_loop(first, last, note, 0)
        n_steps = n_steps + last - first

    def fetch(step):
        tile = steps[step]
        at = lax.rem(tile, tiles) * TILE
        group = lax.div(tile, tiles) * GROUPS + lax.div(at, 128)
        fetch_slabs(
            table_ref, lambda g, lane: lax.shift_right_logical(found_ref[g, lane], 3),
            group, lax.rem(at, 128), slabs, lax.rem(step, SLOTS), slab_sem,
        )

    def first_fetch(step, _):
        fetch(step)
        return 0

    lax.fori_loop(0, jnp.minimum(n_steps, SLOTS - 1), first_fetch, 0)

    def out_copy(step):
        slot = lax.rem(step, 2)
        return pltpu.make_async_copy(
            rows.at[slot], out_ref.at[pl.ds(steps[step] * TILE, TILE), :], row_sem.at[slot]
        )

    def work(step, _):
        @pl.when(step + SLOTS - 1 < n_steps)
        def _():
            fetch(step + SLOTS - 1)

        @pl.when(step >= 2)
        def _():
            out_copy(step - 2).wait()

        base = pl.multiple_of(steps[step] * TILE, TILE)
        pick_rows(picks, base, slabs, lax.rem(step, SLOTS), slab_sem, rows, lax.rem(step, 2))
        out_copy(step).start()
        return 0

    lax.fori_loop(0, n_steps, work, 0)
    for back in (2, 1):
        @pl.when(n_steps >= back)
        def _(back=back):
            out_copy(n_steps - back).wait()


def gather_rows(found, counts, table, per_block):
    dim = table.shape[2]
    smem, vmem = pl.BlockSpec(memory_space=pltpu.SMEM), pl.BlockSpec(memory_space=pltpu.VMEM)
    return pl.pallas_call(
        gather_kernel,
        out_shape=jax.ShapeDtypeStruct((4 * per_block, dim), jnp.bfloat16),
        in_specs=[smem, smem, vmem, pl.BlockSpec(memory_space=pl.ANY)],
        out_specs=pl.BlockSpec(memory_space=pl.ANY),
        scratch_shapes=[
            pltpu.VMEM((4 * per_block, 128), jnp.int32),
            pltpu.VMEM((SLOTS, 8 * TILE, dim), jnp.bfloat16),
            pltpu.VMEM((2, TILE, dim), jnp.bfloat16),
            pltpu.SMEM((4 * per_block // TILE,), jnp.int32),
            pltpu.SemaphoreType.DMA((SLOTS,)),
            pltpu.SemaphoreType.DMA((2,)),
        ],
        compiler_params=pltpu.CompilerParams(vmem_limit_bytes=40 << 20),
        cost_estimate=pl.CostEstimate(flops=1 << 34, bytes_accessed=1 << 26, transcendentals=0),
        name="gather_rows",
    )(found, counts, found, table)


def block_kernel(
    cap, stride, parts, gain_ref, place_ref, counts_ref, part_ref, mine_ref, near_ref, far_ref, rows_ref, w1_ref, w2_ref,
    out_ref, w1p_ref, w2p_ref, sums_ref,
    inbox, ours_rows, normed, kept, acc, w1_buf, w2_buf, sum_buf, out_buf,
    pair_send, pair_recv, load_sem, w_send, w_recv, ready, x_send, x_recv, w_sem, s_send, s_recv, r_sem, o_sem, early_sem,
):
    me, dp = lax.axis_index("tp"), lax.axis_index("dp")
    core = lax.rem(me, 2)
    partner = me + 1 - 2 * core
    other = lax.rem(me + 2, 4)
    dim = gain_ref.shape[1]
    n_tok = out_ref.shape[0]
    width = w1_ref.shape[1]
    w_steps = width // WIDTH
    n_chunks = n_tok // CHUNK
    n_pieces = n_tok // PIECE

    barrier = pltpu.get_barrier_semaphore()
    for peer in (partner, other):
        pl.semaphore_signal(barrier, inc=1, device_id=(dp, peer), device_id_type=MESH)
    pl.semaphore_wait(barrier, 2)

    def remote(src, dst, send, recv, peer):
        return pltpu.make_async_remote_copy(
            src_ref=src, dst_ref=dst, send_sem=send, recv_sem=recv, device_id=(dp, peer), device_id_type=MESH
        )

    own_zone = pl.ds(pl.multiple_of(core * EARLY, EARLY), EARLY)
    partner_zone = pl.ds(pl.multiple_of((1 - core) * EARLY, EARLY), EARLY)

    def pair(i, p, at, n):
        src = pl.ds((1 - p) * stride + at, n)
        return remote(rows_ref.at[src, :], inbox.at[p, pl.ds(at, n), :], pair_send.at[i], pair_recv.at[i], partner)

    def load(i, p, at, n):
        src = pl.ds((3 - p) * stride + at, n)
        return pltpu.make_async_copy(rows_ref.at[src, :], ours_rows.at[1 - p, pl.ds(at, n), :], load_sem.at[i])

    def cross(i, p, at, n):
        span = pl.ds(at, n)
        return remote(ours_rows.at[1 - p, span, :], inbox.at[p, span, :], x_send.at[i], x_recv.at[i], other)

    pair_early = remote(part_ref, inbox.at[0, own_zone, :], early_sem.at[0], early_sem.at[1], partner)
    load_early = pltpu.make_async_copy(mine_ref, ours_rows.at[1, own_zone, :], early_sem.at[2])
    take_early = [
        pltpu.make_async_copy(near_ref, inbox.at[0, own_zone, :], early_sem.at[3]),
        pltpu.make_async_copy(far_ref, inbox.at[0, partner_zone, :], early_sem.at[4]),
    ]

    weights = [
        remote(w1_ref, w1p_ref, w_send.at[0], w_recv.at[0], partner),
        remote(w2_ref, w2p_ref, w_send.at[1], w_recv.at[1], partner),
    ]
    for i, part in enumerate(parts):
        pair(i, *part).start()
        load(i, *part).start()
    pair_early.start()
    load_early.start()
    for copy in weights:
        copy.start()

    def fetch_weights(step, slot, start):
        @pl.when(step < w_steps)
        def _():
            cols = pl.ds(pl.multiple_of(step * WIDTH, WIDTH), WIDTH)
            start(pltpu.make_async_copy(w1_ref.at[:, cols], w1_buf.at[slot], w_sem.at[0, slot]))
            start(pltpu.make_async_copy(w2_ref.at[cols, :], w2_buf.at[slot], w_sem.at[1, slot]))

        @pl.when(step >= w_steps)
        def _():
            cols = pl.ds(pl.multiple_of((step - w_steps) * WIDTH, WIDTH), WIDTH)
            start(pltpu.make_async_copy(w1p_ref.at[:, cols], w1_buf.at[slot], w_sem.at[0, slot]))
            start(pltpu.make_async_copy(w2p_ref.at[cols, :], w2_buf.at[slot], w_sem.at[1, slot]))

    fetch_weights(0, 0, lambda copy: copy.start())

    def merge(p, at, n):
        b = 1 - p
        core0_end = 2 * EARLY + counts_ref[2 * b, 0]
        chip_end = core0_end + counts_ref[2 * b + 1, 0]

        @pl.loop(0, n // 16)
        def _(t):
            base = pl.multiple_of(at + t * 16, 16)
            span = pl.ds(base, 16)
            pos = base + lax.broadcasted_iota(jnp.int32, (16, dim), 0)
            mine = ours_rows[b, span, :].astype(jnp.float32)
            theirs = inbox[p, span, :].astype(jnp.float32)
            if at >= 2 * EARLY:
                from_core0 = pos < core0_end
            else:
                from_core0 = (pos < EARLY) | ((pos >= 2 * EARLY) & (pos < core0_end))
            merged = jnp.where(jnp.where(from_core0, 0, 1) == core, mine, theirs)
            ours_rows[b, span, :] = jnp.where(pos < chip_end, merged, 0.0).astype(jnp.bfloat16)

    for i, part in enumerate(parts):
        load(i, *part).wait()
        pair(i, *part).wait_recv()
        merge(*part)
        pl.semaphore_signal(ready.at[i], inc=1, device_id=(dp, other), device_id_type=MESH)
        pl.semaphore_wait(ready.at[i], 1)
        cross(i, *part).start()
    load_early.wait()
    pair_early.wait_recv()
    merge(0, 0, 2 * EARLY)
    for copy in take_early:
        copy.start()
    for copy in take_early:
        copy.wait()

    gain = gain_ref[...].astype(jnp.float32)

    sums_land = sum_buf if cap < stride else sums_ref

    def send_sums(piece):
        span = pl.ds(pl.multiple_of(piece * PIECE, PIECE), PIECE)
        return remote(acc.at[span, :], sums_land.at[span, :], s_send.at[piece], s_recv.at[piece], other)

    @pl.loop(0, 2)
    def _(b):
        for p in range(2):
            @pl.when(b == p)
            def _(p=p):
                for i, part in enumerate(parts):
                    if part[0] == p:
                        cross(i, *part).wait_recv()

        @pl.loop(0, n_tok // 256)
        def _(t):
            span = pl.ds(pl.multiple_of(t * 256, 256), 256)
            slot = lax.broadcasted_iota(jnp.int32, (128, cap), 1).astype(jnp.float32)
            diagonal = lax.broadcasted_iota(jnp.int32, (128, 128), 0) == lax.broadcasted_iota(
                jnp.int32, (128, 128), 1
            )

            def pick_from(side):
                picks = []
                for g in range(2):
                    row = place_ref[side, pl.ds(b * (n_tok // 128) + 2 * t + g, 1), :]
                    column = jnp.sum(jnp.where(diagonal, row, 0.0), axis=1, keepdims=True)
                    picks.append(ones_where(slot == column))
                return jnp.concatenate(picks, axis=0)

            pick_ours, pick_other = pick_from(0), pick_from(1)
            rows = jnp.dot(pick_ours, ours_rows[b], preferred_element_type=jnp.float32) + jnp.dot(
                pick_other, inbox[b], preferred_element_type=jnp.float32
            )
            kept[span, :] = rows.astype(jnp.bfloat16)
            inv_rms = lax.rsqrt(jnp.mean(rows * rows, axis=-1, keepdims=True) + RMS_EPS)
            normed[span, :] = (rows * inv_rms * gain).astype(jnp.bfloat16)

        @pl.loop(0, n_chunks)
        def _(chunk):
            tok = pl.ds(pl.multiple_of(chunk * CHUNK, CHUNK), CHUNK)
            out_rows = pl.ds(pl.multiple_of(b * n_tok + chunk * CHUNK, CHUNK), CHUNK)
            acc[out_rows, :] = jnp.zeros((CHUNK, dim), jnp.float32)

            @pl.loop(0, 2 * w_steps)
            def _(w):
                step = (b * n_chunks + chunk) * 2 * w_steps + w
                slot = lax.rem(step, 2)
                fetch_weights(w, slot, lambda copy: copy.wait())

                @pl.when(step == w_steps - 1)
                def _():
                    for copy in weights:
                        copy.wait_recv()

                @pl.when(step + 1 < 2 * n_chunks * 2 * w_steps)
                def _():
                    fetch_weights(lax.rem(step + 1, 2 * w_steps), 1 - slot, lambda copy: copy.start())

                parts = []
                for half in range(2):
                    cols = pl.ds(half * (WIDTH // 2), WIDTH // 2)
                    z = jnp.dot(normed[tok, :], w1_buf[slot, :, cols], preferred_element_type=jnp.float32)
                    z = z.astype(jnp.bfloat16).astype(jnp.float32)
                    inner = 0.7978845608028654 * (z + 0.044715 * (z * z * z))
                    parts.append((0.5 * z * (1.0 + jnp.tanh(inner))).astype(jnp.bfloat16))
                hidden = jnp.concatenate(parts, axis=1)
                for half in range(2):
                    cols = pl.ds(half * (dim // 2), dim // 2)
                    acc[out_rows, cols] += jnp.dot(
                        hidden, w2_buf[slot, :, cols], preferred_element_type=jnp.float32
                    )

            @pl.when(b == 0)
            def _():
                for q in range(CHUNK // PIECE):
                    send_sums(chunk * (CHUNK // PIECE) + q).start()

    sums_in_vmem = cap < stride

    def take_sums(piece, slot):
        span = pl.ds(pl.multiple_of(piece * PIECE, PIECE), PIECE)
        return pltpu.make_async_copy(sums_ref.at[span, :], sum_buf.at[slot], r_sem.at[slot])

    def put_out(piece, slot):
        span = pl.ds(pl.multiple_of(piece * PIECE, PIECE), PIECE)
        return pltpu.make_async_copy(out_buf.at[slot], out_ref.at[span, :], o_sem.at[slot])

    @pl.loop(0, n_pieces)
    def _(piece):
        slot = lax.rem(piece, 2)
        send_sums(piece).wait_recv()
        if not sums_in_vmem:
            take = take_sums(piece, slot)
            take.start()
            take.wait()

        @pl.when(piece >= 2)
        def _():
            put_out(piece - 2, slot).wait()

        span = pl.ds(pl.multiple_of(piece * PIECE, PIECE), PIECE)
        own = pl.ds(pl.multiple_of(n_tok + piece * PIECE, PIECE), PIECE)
        total = acc[own, :] + (sums_land[span, :] if sums_in_vmem else sum_buf[slot])
        out_buf[slot] = (kept[span, :].astype(jnp.float32) + total).astype(jnp.bfloat16)
        put_out(piece, slot).start()

    put_out(n_pieces - 2, lax.rem(n_pieces - 2, 2)).wait()
    put_out(n_pieces - 1, lax.rem(n_pieces - 1, 2)).wait()

    sent = [pair(i, *part) for i, part in enumerate(parts)] + [cross(i, *part) for i, part in enumerate(parts)]
    for copy in [pair_early] + sent + weights:
        copy.wait_send()

    @pl.loop(0, n_pieces)
    def _(piece):
        send_sums(piece).wait_send()


def split_rows(p, first, last, ways=4):
    cuts = [first + 16 * ((last - first) // 16 * i // ways) for i in range(ways + 1)]
    return [(p, cuts[i], cuts[i + 1] - cuts[i]) for i in range(ways)]


def mlp_block(packed, collective_id, gain, place, counts, part, mine, near, far, rows, w_in, w_out):
    n_tok = place.shape[1] * 64
    stride = rows.shape[0] // 4
    cap = packed or stride
    parts = split_rows(0, 2 * EARLY, cap) + split_rows(1, 0, cap)
    n_parts = len(parts)
    dim, width = w_in.shape
    any_spec, vmem = pl.BlockSpec(memory_space=pl.ANY), pl.BlockSpec(memory_space=pltpu.VMEM)
    smem = pl.BlockSpec(memory_space=pltpu.SMEM)
    dma = pltpu.SemaphoreType.DMA
    n_pieces = n_tok // PIECE
    flops = 2 * (2 * n_tok) * dim * (2 * width) * 2
    return pl.pallas_call(
        functools.partial(block_kernel, cap, stride, parts),
        out_shape=[
            jax.ShapeDtypeStruct((n_tok, dim), jnp.bfloat16),
            jax.ShapeDtypeStruct(w_in.shape, w_in.dtype),
            jax.ShapeDtypeStruct(w_out.shape, w_out.dtype),
            jax.ShapeDtypeStruct((8 if packed else n_tok, dim), jnp.float32),
        ],
        in_specs=[vmem, vmem, smem] + [any_spec] * 7,
        out_specs=[any_spec] * 4,
        scratch_shapes=[
            pltpu.VMEM((2, cap, dim), jnp.bfloat16),
            pltpu.VMEM((2, cap, dim), jnp.bfloat16),
            pltpu.VMEM((n_tok, dim), jnp.bfloat16),
            pltpu.VMEM((n_tok, dim), jnp.bfloat16),
            pltpu.VMEM((2 * n_tok, dim), jnp.float32),
            pltpu.VMEM((2, dim, WIDTH), jnp.bfloat16),
            pltpu.VMEM((2, WIDTH, dim), jnp.bfloat16),
            pltpu.VMEM((n_tok, dim) if packed else (2, PIECE, dim), jnp.float32),
            pltpu.VMEM((2, PIECE, dim), jnp.bfloat16),
            dma((n_parts,)), dma((n_parts,)), dma((n_parts,)), dma((2,)), dma((2,)),
            pltpu.SemaphoreType.REGULAR((n_parts,)),
            dma((n_parts,)), dma((n_parts,)), dma((2, 2)), dma((n_pieces,)), dma((n_pieces,)), dma((2,)), dma((2,)), dma((5,)),
        ],
        compiler_params=pltpu.CompilerParams(
            collective_id=collective_id, has_side_effects=True, vmem_limit_bytes=67043328
        ),
        cost_estimate=pl.CostEstimate(flops=flops, bytes_accessed=1 << 28, transcendentals=0),
        name="mlp_block",
    )(gain, place, counts, part, mine, near, far, rows, w_in, w_out)[0]


def copy_kernel(src_ref, dst_ref, buf, in_sem, out_sem):
    n = buf.shape[0]
    rows = buf.shape[1]
    ins = [pltpu.make_async_copy(src_ref.at[pl.ds(i * rows, rows), :], buf.at[i], in_sem.at[i]) for i in range(n)]
    outs = [pltpu.make_async_copy(buf.at[i], dst_ref.at[pl.ds(i * rows, rows), :], out_sem.at[i]) for i in range(n)]
    for copy in ins:
        copy.start()
    for i in range(n):
        ins[i].wait()
        outs[i].start()
    for copy in outs:
        copy.wait()


def copy_out(x):
    n = 8
    return pl.pallas_call(
        copy_kernel,
        out_shape=jax.ShapeDtypeStruct(x.shape, x.dtype),
        in_specs=[pl.BlockSpec(memory_space=pl.ANY)],
        out_specs=pl.BlockSpec(memory_space=pl.ANY),
        scratch_shapes=[
            pltpu.VMEM((n, x.shape[0] // n, x.shape[1]), x.dtype),
            pltpu.SemaphoreType.DMA((n,)),
            pltpu.SemaphoreType.DMA((n,)),
        ],
        compiler_params=pltpu.CompilerParams(vmem_limit_bytes=62 << 20),
        name="copy_out",
    )(x)


def solution(mesh):
    swap = [(0, 1), (1, 0)]
    near_pairs = [(r, r ^ 2) for r in range(4)]
    far_pairs = [(r, r ^ 3) for r in range(4)]

    def device_step(token_ids, table_shard, norm_gain, w_in_shard, w_out_shard):
        shard_rows, dim = table_shard.shape
        n_tok = token_ids.shape[0] // 4
        by_block = token_ids.reshape(4, n_tok)
        above = [n_tok] + [jnp.sum((by_block >= q * shard_rows).astype(jnp.int32), axis=1) for q in (1, 2, 3)] + [0]
        rest = [jnp.maximum(above[q] - above[q + 1] - EARLY, 0) for q in range(4)]
        need = 2 * EARLY + jnp.max(jnp.maximum(rest[0] + rest[1], rest[2] + rest[3])).reshape(1)
        need = jnp.maximum(need, lax.ppermute(need, "dp", swap))[0]

        table = table_shard.reshape(-1, 8, dim)
        part, mine, found, place, counts, rests = early_rows(token_ids, table)
        near = lax.ppermute(mine, "tp", near_pairs)
        far = lax.ppermute(part, "tp", far_pairs)
        rows = gather_rows(found, counts, table, -(-(n_tok + EARLY) // 128) * 128)
        out = lax.switch(
            sum((need > cap).astype(jnp.int32) for cap in PACKED),
            [functools.partial(mlp_block, cap, i) for i, cap in enumerate(PACKED + (None,))],
            norm_gain[None, :], place, rests, part, mine, near, far, rows, w_in_shard, w_out_shard,
        )
        return copy_out(out)

    return jax.shard_map(
        device_step,
        mesh=mesh,
        in_specs=(P("dp"), P("tp", None), P(), P(None, "tp"), P("tp", None)),
        out_specs=P(("dp", "tp"), None),
        check_vma=False,
    )
```

time: 358 us -> 331 us (0.925); the launches traced: 357 us -> 334 us
  Pallas kernels: 348 us -> 324 us
    pallas_call x2 -> x3, Pallas kernels: 344 us -> 320 us  [the longest x1 283 us: mlp_block(): pl.pallas_call(functools.partial(block_kernel, cap, stride, parts), out_s...]
  transfers between devices with their start and end apart: 1 -> 3, of which waited for: 0 -> 0; matrix products, arithmetic and copies ran while one was open for 0% -> 0% of each run, Pallas kernels for 9% -> 11%
where the time goes in v4:
time: 331 us; the launch traced here: 334 us
  Pallas kernels  324 us (98%)
  starting transfers between devices  5.98 us (2%)
    pallas_call x1, Pallas kernels, mlp_block(): pl.pallas_call(functools.partial(block_kernel, cap, stride, parts), out_s...  283 us
    pallas_call x1, Pallas kernels, gather_rows(): pl.pallas_call(gather_kernel, out_shape=jax.ShapeDtypeStruct((4 * per_blo...  29.7 us
    pallas_call x1, Pallas kernels, early_rows(): pl.pallas_call(functools.partial(early_kernel, 8 * slab_count), out_shape...  7.86 us
  transfers between devices with their start and end apart: 3, of which 0 were waited for; matrix products, arithmetic and copies ran while one was open for 0% of the time, Pallas kernels for 11%

profile of v4, /device:TPU:0, one launch (start us, length us, event | category | flops | bytes accessed | tf_op | source)
XLA Modules:
  0.0 334.5 jit_solution(835477903057564039)
XLA Ops:
  0.0 0.7 compare_convert_fusion.2
  0.7 0.1 reduce_sum.27
  0.9 0.1 reduce_sum.28
  1.0 0.1 reduce_sum.29
  1.1 0.6 maximum_reduce_fusion
  2.4 4.7 %collective-permute-start = (s32[1]{0:T(128)}, s32[1]{0:T(128)}, u32[]{:S(2)}, u32[]{:S(2)}) collective-permute-start(s32[1]{0:T(128)} %bitcast), channel_id=1, source_target_pairs={{0,4},{4,0},{1,5},{5,1},{2,6},{6,2},{3,7},{7,3}} | collective-permute-start | bytes 20 | tf_op jit(solution)/shard_map/ppermute | solution.py:599
  7.1 0.0 copy-start
  7.1 0.7 copy-done
  7.8 7.9 %early_rows.1 = (bf16[128,2048]{1,0:T(8,128)(2,1)}, bf16[128,2048]{1,0:T(8,128)(2,1)}, s32[64,128]{1,0:T(8,128)S(1)}, f32[2,16,128]{2,1,0:T(8,128)}, s32[64,128]{1,0:T(8,128)S(1)}, /*index=5*/s32[4,128]{1,0:T(4,128)}) custom-call(s32[32,128]{1,0:T(8,128)S(1)} %bitcast.4, bf16[8000,8,2048]{2,1,0:T(8,128)(2,1)} %bitcast.3.table_ref), custom_call_target="tpu_custom_call" | custom-call | flops 4294967296 | bytes 33554432 | tf_op jit(solution)/shard_map/early_rows/pallas_call | solution.py:150
  15.7 0.0 collective-permute-start.2
  15.7 1.3 collective-permute-start.1
  17.0 0.0 copy-start.1
  17.0 29.7 %gather_rows.1 = bf16[4608,2048]{1,0:T(8,128)(2,1)} custom-call(s32[64,128]{1,0:T(8,128)S(1)} %get-tuple-element.112.found_ref.found_vmem, s32[64,128]{1,0:T(8,128)S(1)} %get-tuple-element.113.counts_ref, s32[64,128]{1,0:T(8,128)S(1)} %get-tuple-element.112.found_ref.found_vmem, bf16[8000,8,2048]{2,1,0:T(8,128)(2,1)} %bitcast.3.table_ref), custom_call_target="tpu_custom_call" | custom-call | flops 17179869184 | bytes 67108864 | tf_op jit(solution)/shard_map/gather_rows/pallas_call | solution.py:256
  46.7 0.0 copy-done.1
  46.7 0.6 broadcast_in_dim.3
  47.3 0.0 collective-permute-done
  47.8 0.0 collective-permute-done.2
  47.9 0.0 collective-permute-done.1
  47.9 282.8 %conditional.1 = (bf16[1024,2048]{1,0:T(8,128)(2,1)}) conditional(s32[]{:T(128)} %bitcast.1, (bf16[1,2048]{1,0:T(2,128)(2,1)}, f32[2,16,128]{2,1,0:T(8,128)}, s32[4,128]{1,0:T(4,128)}, bf16[128,2048]{1,0:T(8,128)(2,1)}, bf16[128,2048]{1,0:T(8,128)(2,1)}, /*index=5*/bf16[128,2048]{1,0:T(8,128)(2,1)}, bf16[128,2048]{1,0:T(8,128)(2,1)}, ...), branch_computations={%region_4.0_spmd, %region_5.0_spmd, %region_6.0_spmd} | conditional | flops 137438953472 | bytes 268435456 | solution.py:606
  47.9 282.6 %mlp_block.3 = (bf16[1024,2048]{1,0:T(8,128)(2,1)}, bf16[2048,4096]{1,0:T(8,128)(2,1)}, bf16[4096,2048]{1,0:T(8,128)(2,1)}, f32[8,2048]{1,0:T(8,128)}) custom-call(bf16[1,2048]{1,0:T(2,128)(2,1)} %get-tuple-element.68.gain_ref, f32[2,16,128]{2,1,0:T(8,128)} %get-tuple-element.70.place_ref, s32[4,128]{1,0:T(4,128)} %get-tuple-element.71.counts_ref, ...), custom_call_target="tpu_custom_call" | custom-call | flops 137438953472 | bytes 268435456 | tf_op jit(solution)/shard_map/cond/branch_0_fun/mlp_block/pallas_call | solution.py:524
  330.7 3.6 %copy_out.1 = bf16[1024,2048]{1,0:T(8,128)(2,1)} custom-call(bf16[1024,2048]{1,0:T(8,128)(2,1)} %get-tuple-element.117.src_ref), custom_call_target="tpu_custom_call" | custom-call | tf_op jit(solution)/shard_map/copy_out/pallas_call | solution.py:572
  (3 shorter events, 0.0 us)
Async XLA Ops:
  2.4 44.9 %collective-permute-start = (s32[1]{0:T(128)}, s32[1]{0:T(128)}, u32[]{:S(2)}, u32[]{:S(2)}) collective-permute-start(s32[1]{0:T(128)} %bitcast), channel_id=1, source_target_pairs={{0,4},{4,0},{1,5},{5,1},{2,6},{6,2},{3,7},{7,3}} | collective-permute-start | bytes 20 | tf_op jit(solution)/shard_map/ppermute | solution.py:599
  7.1 0.7 copy-start
  15.7 32.1 %collective-permute-start.2 = (bf16[128,2048]{1,0:T(8,128)(2,1)}, bf16[128,2048]{1,0:T(8,128)(2,1)}, u32[]{:S(2)}, u32[]{:S(2)}) collective-permute-start(bf16[128,2048]{1,0:T(8,128)(2,1)} %get-tuple-element.110), channel_id=1, source_target_pairs={{0,3},{1,2},{2,1},{3,0},{4,7},{5,6},{6,5},{7,4}} | collective-permute-start | bytes 1572872 | tf_op jit(solution)/shard_map/ppermute | solution.py:604
  15.7 32.1 %collective-permute-start.1 = (bf16[128,2048]{1,0:T(8,128)(2,1)}, bf16[128,2048]{1,0:T(8,128)(2,1)}, u32[]{:S(2)}, u32[]{:S(2)}) collective-permute-start(bf16[128,2048]{1,0:T(8,128)(2,1)} %get-tuple-element.111), channel_id=1, source_target_pairs={{0,2},{1,3},{2,0},{3,1},{4,6},{5,7},{6,4},{7,5}} | collective-permute-start | bytes 1572872 | tf_op jit(solution)/shard_map/ppermute | solution.py:603
  17.0 29.7 %copy-start.1 = (bf16[2048]{0:T(1024)(128)(2,1)S(1)}, bf16[2048]{0:T(1024)(128)(2,1)}, u32[]{:S(2)}) copy-start(bf16[2048]{0:T(1024)(128)(2,1)} %param.10) | copy-start | bytes 12292

commit v5 on v4

--- a/solution.py
+++ b/solution.py
@@ -11,7 +11,7 @@
 TILE = 64
 PICK = 32
 SLOTS = 4
-EARLY = 128
+EARLY = 192
 GROUPS = 16
 PIECE = 128
 CHUNK = 512
@@ -55,7 +55,7 @@
 
 
 def early_kernel(
-    shard_rows, tokens_ref, table_ref, part_ref, mine_ref, found_ref, place_ref, counts_ref, rests_ref,
+    shard_rows, tokens_ref, table_ref, part_ref, mine_ref, found_ref, place_ref, counts_ref, need_ref,
     slab_no, slab_no_smem, picks, slabs, rows, meta_sem, slab_sem, row_sem,
 ):
     me = lax.axis_index("tp")
@@ -88,12 +88,11 @@
     ours = lax.shift_right_logical(owner, 1) == chip
     place_ref[0] = jnp.where(ours, place, -1)[groups // 2:].astype(jnp.float32)
     place_ref[1] = jnp.where(ours, -1, place)[groups // 2:].astype(jnp.float32)
-    counts_ref[pl.ds(0, groups), :] = jnp.where(chip == 0, rest[0], rest[2]).astype(jnp.int32)
-    counts_ref[pl.ds(groups, groups), :] = jnp.where(chip == 0, rest[1], rest[3]).astype(jnp.int32)
-
-    for i in range(4):
-        row = (i % 2) * groups + (2 + i // 2) * per
-        rests_ref[pl.ds(i, 1), :] = counts_ref[pl.ds(row, 1), :]
+    for i, rests in enumerate((jnp.where(chip == 0, rest[0], rest[2]), jnp.where(chip == 0, rest[1], rest[3]))):
+        for b in range(4):
+            counts_ref[pl.ds(4 * i + b, 1), :] = rests[b * per:b * per + 1].astype(jnp.int32)
+    need = jnp.max(jnp.maximum(rest[0] + rest[1], rest[2] + rest[3]), axis=0, keepdims=True)
+    need_ref[...] = need.astype(jnp.int32) + 2 * EARLY
 
     mine = owner == me
     local = jnp.where(mine, ids - me * shard_rows, 0)
@@ -102,23 +101,27 @@
     eye = ones_where(r == c)
     lane_of = to_column(eye, place & 127)
     group_row = lax.broadcasted_iota(jnp.int32, (GROUPS, 128), 0)
-    for b in (1, 3, 0, 2):
+
+    def find(b):
         acc = jnp.zeros((2 * GROUPS, 128), jnp.float32)
         for g in range(b * per, (b + 1) * per):
             hit = (place_group[g:g + 1] == group_row) & mine[g:g + 1]
             lhs = jnp.concatenate([jnp.where(hit, high[g:g + 1], 0.0), jnp.where(hit, low[g:g + 1], 0.0)], axis=0)
             acc = acc + exact_dot(lhs, ones_where(lane_of[:, g:g + 1] == c))
-        found_ref[pl.ds(b * GROUPS, GROUPS), :] = (acc[:GROUPS] * 256.0 + acc[GROUPS:]).astype(jnp.int32)
+        found = (acc[:GROUPS] * 256.0 + acc[GROUPS:]).astype(jnp.int32)
+        found_ref[pl.ds(b * GROUPS, GROUPS), :] = found
+        return found
 
     early_groups = 2 * EARLY // 128
-    for i, b in enumerate((1, 3)):
-        found = found_ref[pl.ds(b * GROUPS, GROUPS), :]
-        slab_no[pl.ds(i * GROUPS, GROUPS), :] = lax.shift_right_logical(found, 3)
-        row_of = to_column(eye, found & 7)
+    firsts = [find(b)[:early_groups] for b in (1, 3)]
+    for i, first in enumerate(firsts):
+        slab_no[pl.ds(i * early_groups, early_groups), :] = lax.shift_right_logical(first, 3)
+    to_smem = pltpu.make_async_copy(slab_no, slab_no_smem, meta_sem)
+    to_smem.start()
+    for i, first in enumerate(firsts):
+        row_of = to_column(eye, first & 7)
         for g in range(early_groups):
             picks[pl.ds((i * early_groups + g) * 128, 128), :] = jnp.broadcast_to(row_of[:, g:g + 1], (128, 128))
-    to_smem = pltpu.make_async_copy(slab_no, slab_no_smem, meta_sem)
-    to_smem.start()
     to_smem.wait()
 
     n = EARLY // TILE
@@ -127,8 +130,10 @@
             at = core * EARLY + t * TILE
             fetch_slabs(
                 table_ref, lambda group, lane: slab_no_smem[group, lane],
-                i * GROUPS + lax.div(at, 128), lax.rem(at, 128), slabs, i * n + t, slab_sem,
+                i * early_groups + lax.div(at, 128), lax.rem(at, 128), slabs, i * n + t, slab_sem,
             )
+    for b in (0, 2):
+        find(b)
     outs = []
     for i in range(2):
         for t in range(n):
@@ -153,14 +158,14 @@
             rows, rows,
             jax.ShapeDtypeStruct((4 * GROUPS, 128), jnp.int32),
             jax.ShapeDtypeStruct((2, groups // 2, 128), jnp.float32),
-            jax.ShapeDtypeStruct((2 * groups, 128), jnp.int32),
-            jax.ShapeDtypeStruct((4, 128), jnp.int32),
+            jax.ShapeDtypeStruct((8, 128), jnp.int32),
+            jax.ShapeDtypeStruct((1, 128), jnp.int32),
         ],
         in_specs=[vmem, any_spec],
         out_specs=[any_spec, any_spec, vmem, vmem, vmem, vmem],
         scratch_shapes=[
-            pltpu.VMEM((2 * GROUPS, 128), jnp.int32),
-            pltpu.SMEM((2 * GROUPS, 128), jnp.int32),
+            pltpu.VMEM((8, 128), jnp.int32),
+            pltpu.SMEM((8, 128), jnp.int32),
             pltpu.VMEM((4 * EARLY, 128), jnp.int32),
             pltpu.VMEM((steps, 8 * TILE, dim), jnp.bfloat16),
             pltpu.VMEM((steps, TILE, dim), jnp.bfloat16),
@@ -174,9 +179,11 @@
     )(token_ids.reshape(groups, 128), table)
 
 
-def gather_kernel(found_ref, counts_ref, found_vmem, table_ref, out_ref, picks, slabs, rows, steps, slab_sem, row_sem):
+def gather_kernel(
+    found_ref, counts_ref, found_vmem, need_in, table_ref, out_ref, need_ref, picks, slabs, rows, steps, slab_sem, row_sem,
+):
+    need_ref[...] = need_in[...]
     core = lax.rem(lax.axis_index("tp"), 2)
-    half = counts_ref.shape[0] // 2
     eye = ones_where(
         lax.broadcasted_iota(jnp.int32, (128, 128), 0) == lax.broadcasted_iota(jnp.int32, (128, 128), 1)
     )
@@ -191,7 +198,7 @@
     tiles = per_block // TILE
     n_steps = 0
     for b in (1, 3, 0, 2):
-        rest0, rest1 = counts_ref[b * (half // 4), 0], counts_ref[half + b * (half // 4), 0]
+        rest0, rest1 = counts_ref[b, 0], counts_ref[4 + b, 0]
         start = jnp.where(core == 0, 2 * EARLY, 2 * EARLY + rest0)
         end = jnp.where(core == 0, 2 * EARLY + rest0, 2 * EARLY + rest0 + rest1)
         if b % 2 == 0:
@@ -250,14 +257,17 @@
             out_copy(n_steps - back).wait()
 
 
-def gather_rows(found, counts, table, per_block):
+def gather_rows(found, counts, need, table, per_block):
     dim = table.shape[2]
     smem, vmem = pl.BlockSpec(memory_space=pltpu.SMEM), pl.BlockSpec(memory_space=pltpu.VMEM)
     return pl.pallas_call(
         gather_kernel,
-        out_shape=jax.ShapeDtypeStruct((4 * per_block, dim), jnp.bfloat16),
-        in_specs=[smem, smem, vmem, pl.BlockSpec(memory_space=pl.ANY)],
-        out_specs=pl.BlockSpec(memory_space=pl.ANY),
+        out_shape=[
+            jax.ShapeDtypeStruct((4 * per_block, dim), jnp.bfloat16),
+            jax.ShapeDtypeStruct(need.shape, need.dtype),
+        ],
+        in_specs=[smem, smem, vmem, vmem, pl.BlockSpec(memory_space=pl.ANY)],
+        out_specs=[pl.BlockSpec(memory_space=pl.ANY), vmem],
         scratch_shapes=[
             pltpu.VMEM((4 * per_block, 128), jnp.int32),
             pltpu.VMEM((SLOTS, 8 * TILE, dim), jnp.bfloat16),
@@ -269,11 +279,92 @@
         compiler_params=pltpu.CompilerParams(vmem_limit_bytes=40 << 20),
         cost_estimate=pl.CostEstimate(flops=1 << 34, bytes_accessed=1 << 26, transcendentals=0),
         name="gather_rows",
-    )(found, counts, found, table)
+    )(found, counts, found, need, table)
+
+
+def merge_into(mine_ref, theirs_ref, at, n, place, rest0, rest1, core):
+    core0_end = 2 * EARLY + rest0
+    chip_end = core0_end + rest1
+    dim = mine_ref.shape[1]
+
+    @pl.loop(0, n // 16)
+    def _(t):
+        span = pl.ds(pl.multiple_of(at + t * 16, 16), 16)
+        pos = place + t * 16 + lax.broadcasted_iota(jnp.int32, (16, dim), 0)
+        from_core0 = pos < core0_end
+        if place < 2 * EARLY:
+            from_core0 = (pos < EARLY) | ((pos >= 2 * EARLY) & from_core0)
+        merged = jnp.where(
+            jnp.where(from_core0, 0, 1) == core,
+            mine_ref[span, :].astype(jnp.float32), theirs_ref[span, :].astype(jnp.float32),
+        )
+        mine_ref[span, :] = jnp.where(pos < chip_end, merged, 0.0).astype(jnp.bfloat16)
+
+
+def merge_kernel(stride, counts_ref, rows_ref, out_ref, mine, theirs, send, recv, load_sem, out_sem):
+    me, dp = lax.axis_index("tp"), lax.axis_index("dp")
+    core = lax.rem(me, 2)
+    partner = me + 1 - 2 * core
+    barrier = pltpu.get_barrier_semaphore()
+    pl.semaphore_signal(barrier, inc=1, device_id=(dp, partner), device_id_type=MESH)
+    n, ways = mine.shape[0], send.shape[0]
+    size = n // ways
+    loads = [
+        pltpu.make_async_copy(
+            rows_ref.at[pl.ds(3 * stride + 2 * EARLY + i * size, size), :], mine.at[pl.ds(i * size, size), :],
+            load_sem.at[i],
+        )
+        for i in range(ways)
+    ]
+    for copy in loads:
+        copy.start()
+    pl.semaphore_wait(barrier, 1)
+    pair = [
+        pltpu.make_async_remote_copy(
+            src_ref=rows_ref.at[pl.ds(stride + 2 * EARLY + i * size, size), :],
+            dst_ref=theirs.at[pl.ds(i * size, size), :],
+            send_sem=send.at[i], recv_sem=recv.at[i], device_id=(dp, partner), device_id_type=MESH,
+        )
+        for i in range(ways)
+    ]
+    outs = [
+        pltpu.make_async_copy(
+            mine.at[pl.ds(i * size, size), :], out_ref.at[pl.ds(i * size, size), :], out_sem.at[i]
+        )
+        for i in range(ways)
+    ]
+    for copy in pair:
+        copy.start()
+    for i in range(ways):
+        loads[i].wait()
+        pair[i].wait_recv()
+        merge_into(mine, theirs, i * size, size, 2 * EARLY + i * size, counts_ref[3, 0], counts_ref[7, 0], core)
+        outs[i].start()
+    for copy in outs:
+        copy.wait()
+    for copy in pair:
+        copy.wait_send()
+
+
+def merge_rows(counts, rows):
+    n, dim, ways = max(PACKED) - 2 * EARLY, rows.shape[1], 4
+    dma = pltpu.SemaphoreType.DMA
+    return pl.pallas_call(
+        functools.partial(merge_kernel, rows.shape[0] // 4),
+        out_shape=jax.ShapeDtypeStruct((n, dim), jnp.bfloat16),
+        in_specs=[pl.BlockSpec(memory_space=pltpu.SMEM), pl.BlockSpec(memory_space=pl.ANY)],
+        out_specs=pl.BlockSpec(memory_space=pl.ANY),
+        scratch_shapes=[pltpu.VMEM((n, dim), jnp.bfloat16)] * 2 + [dma((ways,))] * 4,
+        compiler_params=pltpu.CompilerParams(
+            collective_id=len(PACKED) + 1, has_side_effects=True, vmem_limit_bytes=16 << 20
+        ),
+        cost_estimate=pl.CostEstimate(flops=1 << 30, bytes_accessed=1 << 23, transcendentals=0),
+        name="merge_rows",
+    )(counts, rows)
 
 
 def block_kernel(
-    cap, stride, parts, gain_ref, place_ref, counts_ref, part_ref, mine_ref, near_ref, far_ref, rows_ref, w1_ref, w2_ref,
+    cap, stride, parts, gain_ref, place_ref, counts_ref, part_ref, mine_ref, near_ref, far_ref, merged_ref, rows_ref, w1_ref, w2_ref,
     out_ref, w1p_ref, w2p_ref, sums_ref,
     inbox, ours_rows, normed, kept, acc, w1_buf, w2_buf, sum_buf, out_buf,
     pair_send, pair_recv, load_sem, w_send, w_recv, ready, x_send, x_recv, w_sem, s_send, s_recv, r_sem, o_sem, early_sem,
@@ -282,7 +373,7 @@
     core = lax.rem(me, 2)
     partner = me + 1 - 2 * core
     other = lax.rem(me + 2, 4)
-    dim = gain_ref.shape[1]
+    dim = w1_ref.shape[0]
     n_tok = out_ref.shape[0]
     width = w1_ref.shape[1]
     w_steps = width // WIDTH
@@ -325,9 +416,21 @@
         remote(w1_ref, w1p_ref, w_send.at[0], w_recv.at[0], partner),
         remote(w2_ref, w2p_ref, w_send.at[1], w_recv.at[1], partner),
     ]
+    late = cap - 2 * EARLY
+    late_zone = pl.ds(2 * EARLY, late)
+    late_cross = remote(
+        merged_ref.at[pl.ds(0, late), :], inbox.at[0, late_zone, :], early_sem.at[5], early_sem.at[6], other
+    ) if cap < stride else None
+    late_load = pltpu.make_async_copy(
+        merged_ref.at[pl.ds(0, late), :], ours_rows.at[1, late_zone, :], early_sem.at[7]
+    ) if cap < stride else None
+    if late_cross is not None:
+        late_cross.start()
     for i, part in enumerate(parts):
         pair(i, *part).start()
         load(i, *part).start()
+    if late_load is not None:
+        late_load.start()
     pair_early.start()
     load_early.start()
     for copy in weights:
@@ -350,22 +453,9 @@
 
     def merge(p, at, n):
         b = 1 - p
-        core0_end = 2 * EARLY + counts_ref[2 * b, 0]
-        chip_end = core0_end + counts_ref[2 * b + 1, 0]
-
-        @pl.loop(0, n // 16)
-        def _(t):
-            base = pl.multiple_of(at + t * 16, 16)
-            span = pl.ds(base, 16)
-            pos = base + lax.broadcasted_iota(jnp.int32, (16, dim), 0)
-            mine = ours_rows[b, span, :].astype(jnp.float32)
-            theirs = inbox[p, span, :].astype(jnp.float32)
-            if at >= 2 * EARLY:
-                from_core0 = pos < core0_end
-            else:
-                from_core0 = (pos < EARLY) | ((pos >= 2 * EARLY) & (pos < core0_end))
-            merged = jnp.where(jnp.where(from_core0, 0, 1) == core, mine, theirs)
-            ours_rows[b, span, :] = jnp.where(pos < chip_end, merged, 0.0).astype(jnp.bfloat16)
+        merge_into(
+            ours_rows.at[b], inbox.at[p], at, n, at, counts_ref[2 + b, 0], counts_ref[6 + b, 0], core
+        )
 
     for i, part in enumerate(parts):
         load(i, *part).wait()
@@ -381,8 +471,11 @@
         copy.start()
     for copy in take_early:
         copy.wait()
-
-    gain = gain_ref[...].astype(jnp.float32)
+    if late_load is not None:
+        late_load.wait()
+
+    gain_rows = gain_ref[...].astype(jnp.float32)
+    gain = jnp.concatenate([gain_rows[i:i + 1] for i in range(gain_ref.shape[0])], axis=1)
 
     sums_land = sum_buf if cap < stride else sums_ref
 
@@ -395,6 +488,8 @@
         for p in range(2):
             @pl.when(b == p)
             def _(p=p):
+                if p == 0 and late_cross is not None:
+                    late_cross.wait_recv()
                 for i, part in enumerate(parts):
                     if part[0] == p:
                         cross(i, *part).wait_recv()
@@ -496,6 +591,8 @@
     put_out(n_pieces - 1, lax.rem(n_pieces - 1, 2)).wait()
 
     sent = [pair(i, *part) for i, part in enumerate(parts)] + [cross(i, *part) for i, part in enumerate(parts)]
+    if late_cross is not None:
+        sent.append(late_cross)
     for copy in [pair_early] + sent + weights:
         copy.wait_send()
 
@@ -509,11 +606,11 @@
     return [(p, cuts[i], cuts[i + 1] - cuts[i]) for i in range(ways)]
 
 
-def mlp_block(packed, collective_id, gain, place, counts, part, mine, near, far, rows, w_in, w_out):
+def mlp_block(packed, collective_id, gain, place, counts, part, mine, near, far, merged, rows, w_in, w_out):
     n_tok = place.shape[1] * 64
     stride = rows.shape[0] // 4
     cap = packed or stride
-    parts = split_rows(0, 2 * EARLY, cap) + split_rows(1, 0, cap)
+    parts = ([] if packed else split_rows(0, 2 * EARLY, cap)) + split_rows(1, 0, cap)
     n_parts = len(parts)
     dim, width = w_in.shape
     any_spec, vmem = pl.BlockSpec(memory_space=pl.ANY), pl.BlockSpec(memory_space=pltpu.VMEM)
@@ -529,7 +626,7 @@
             jax.ShapeDtypeStruct(w_out.shape, w_out.dtype),
             jax.ShapeDtypeStruct((8 if packed else n_tok, dim), jnp.float32),
         ],
-        in_specs=[vmem, vmem, smem] + [any_spec] * 7,
+        in_specs=[vmem, vmem, smem] + [any_spec] * 8,
         out_specs=[any_spec] * 4,
         scratch_shapes=[
             pltpu.VMEM((2, cap, dim), jnp.bfloat16),
@@ -543,14 +640,14 @@
             pltpu.VMEM((2, PIECE, dim), jnp.bfloat16),
             dma((n_parts,)), dma((n_parts,)), dma((n_parts,)), dma((2,)), dma((2,)),
             pltpu.SemaphoreType.REGULAR((n_parts,)),
-            dma((n_parts,)), dma((n_parts,)), dma((2, 2)), dma((n_pieces,)), dma((n_pieces,)), dma((2,)), dma((2,)), dma((5,)),
+            dma((n_parts,)), dma((n_parts,)), dma((2, 2)), dma((n_pieces,)), dma((n_pieces,)), dma((2,)), dma((2,)), dma((8,)),
         ],
         compiler_params=pltpu.CompilerParams(
             collective_id=collective_id, has_side_effects=True, vmem_limit_bytes=67043328
         ),
         cost_estimate=pl.CostEstimate(flops=flops, bytes_accessed=1 << 28, transcendentals=0),
         name="mlp_block",
-    )(gain, place, counts, part, mine, near, far, rows, w_in, w_out)[0]
+    )(gain, place, counts, part, mine, near, far, merged, rows, w_in, w_out)[0]
 
 
 def copy_kernel(src_ref, dst_ref, buf, in_sem, out_sem):
@@ -592,21 +689,17 @@
     def device_step(token_ids, table_shard, norm_gain, w_in_shard, w_out_shard):
         shard_rows, dim = table_shard.shape
         n_tok = token_ids.shape[0] // 4
-        by_block = token_ids.reshape(4, n_tok)
-        above = [n_tok] + [jnp.sum((by_block >= q * shard_rows).astype(jnp.int32), axis=1) for q in (1, 2, 3)] + [0]
-        rest = [jnp.maximum(above[q] - above[q + 1] - EARLY, 0) for q in range(4)]
-        need = 2 * EARLY + jnp.max(jnp.maximum(rest[0] + rest[1], rest[2] + rest[3])).reshape(1)
-        need = jnp.maximum(need, lax.ppermute(need, "dp", swap))[0]
-
         table = table_shard.reshape(-1, 8, dim)
-        part, mine, found, place, counts, rests = early_rows(token_ids, table)
+        part, mine, found, place, counts, need = early_rows(token_ids, table)
         near = lax.ppermute(mine, "tp", near_pairs)
         far = lax.ppermute(part, "tp", far_pairs)
-        rows = gather_rows(found, counts, table, -(-(n_tok + EARLY) // 128) * 128)
+        rows, need = gather_rows(found, counts, need, table, -(-(n_tok + EARLY) // 128) * 128)
+        merged = merge_rows(counts, rows)
+        need = jnp.maximum(need, lax.ppermute(need, "dp", swap))[0, 0]
         out = lax.switch(
             sum((need > cap).astype(jnp.int32) for cap in PACKED),
             [functools.partial(mlp_block, cap, i) for i, cap in enumerate(PACKED + (None,))],
-            norm_gain[None, :], place, rests, part, mine, near, far, rows, w_in_shard, w_out_shard,
+            norm_gain.reshape(-1, 128), place, counts, part, mine, near, far, merged, rows, w_in_shard, w_out_shard,
         )
         return copy_out(out)
 

time: 331 us -> 322 us (0.973); the launches traced: 334 us -> 322 us
  Pallas kernels: 324 us -> 313 us
  waiting for transfers between devices: 0.01 us -> 3.72 us
    pallas_call x1, Pallas kernels: 283 us -> 270 us  [mlp_block(): pl.pallas_call(functools.partial(block_kernel, cap, stride, parts), out_s...]
    ppermute x1, starting transfers between devices: 4.69 us -> 0.03 us  [device_step(): need = jnp.maximum(need, lax.ppermute(need, 'dp', swap))[0, 0]]
    ppermute x1, waiting for transfers between devices: 0.01 us -> 3.71 us  [device_step(): near = lax.ppermute(mine, 'tp', near_pairs)]
    pallas_call x1 -> x2, Pallas kernels: 29.7 us -> 30.5 us  [the longest x1 25.7 us: gather_rows(): pl.pallas_call(gather_kernel, out_shape=[jax.ShapeDtypeStruct((4 * per_bl...]
  transfers between devices with their start and end apart: 3 -> 3, of which waited for: 0 -> 1; matrix products, arithmetic and copies ran while one was open for 0% -> 0% of each run, Pallas kernels for 11% -> 9%
where the time goes in v5:
time: 322 us
  Pallas kernels  313 us (97%)
  waiting for transfers between devices  3.72 us (1%)
  starting transfers between devices  3.29 us (1%)
    pallas_call x1, Pallas kernels, mlp_block(): pl.pallas_call(functools.partial(block_kernel, cap, stride, parts), out_s...  270 us
    pallas_call x1, Pallas kernels, gather_rows(): pl.pallas_call(gather_kernel, out_shape=[jax.ShapeDtypeStruct((4 * per_bl...  25.7 us
    pallas_call x1, Pallas kernels, early_rows(): pl.pallas_call(functools.partial(early_kernel, 8 * slab_count), out_shape...  9.26 us
  transfers between devices with their start and end apart: 3, of which 1 were waited for; matrix products, arithmetic and copies ran while one was open for 0% of the time, Pallas kernels for 9%

profile of v5, /device:TPU:0, one launch (start us, length us, event | category | flops | bytes accessed | tf_op | source)
XLA Modules:
  0.0 321.7 jit_solution(18148884020925423180)
XLA Ops:
  0.0 0.0 copy-start
  0.0 0.7 copy-done
  0.7 9.3 %early_rows.1 = (bf16[192,2048]{1,0:T(8,128)(2,1)}, bf16[192,2048]{1,0:T(8,128)(2,1)}, s32[64,128]{1,0:T(8,128)S(1)}, f32[2,16,128]{2,1,0:T(8,128)}, s32[8,128]{1,0:T(8,128)}, /*index=5*/s32[1,128]{1,0:T(1,128)S(1)}) custom-call(s32[32,128]{1,0:T(8,128)S(1)} %bitcast.5, bf16[8000,8,2048]{2,1,0:T(8,128)(2,1)} %bitcast.1.table_ref), custom_call_target="tpu_custom_call" | custom-call | flops 4294967296 | bytes 33554432 | tf_op jit(solution)/shard_map/early_rows/pallas_call | solution.py:155
  10.0 2.7 collective-permute-start.2
  12.7 0.6 collective-permute-start.1
  13.3 25.7 %gather_rows.1 = (bf16[5120,2048]{1,0:T(8,128)(2,1)}, s32[1,128]{1,0:T(1,128)S(1)}) custom-call(s32[64,128]{1,0:T(8,128)S(1)} %get-tuple-element.119.found_ref.found_vmem, s32[8,128]{1,0:T(8,128)} %get-tuple-element.120.counts_ref, s32[64,128]{1,0:T(8,128)S(1)} %get-tuple-element.119.found_ref.found_vmem, s32[1,128]{1,0:T(1,128)S(1)} %get-tuple-element.121.need_in, ...), custom_call_target="tpu_custom_call" | custom-call | flops 17179869184 | bytes 67108864 | tf_op jit(solution)/shard_map/gather_rows/pallas_call | solution.py:263
  39.0 0.0 collective-permute-start
  39.0 4.8 %merge_rows.1 = bf16[320,2048]{1,0:T(8,128)(2,1)} custom-call(s32[8,128]{1,0:T(8,128)} %get-tuple-element.120.counts_ref, bf16[5120,2048]{1,0:T(8,128)(2,1)} %get-tuple-element.126.rows_ref), custom_call_target="tpu_custom_call" | custom-call | flops 1073741824 | bytes 8388608 | tf_op jit(solution)/shard_map/merge_rows/pallas_call | solution.py:352
  43.8 0.0 collective-permute-done
  43.9 0.0 collective-permute-done.2
  43.9 3.7 %collective-permute-done.1 = bf16[192,2048]{1,0:T(8,128)(2,1)} collective-permute-done((bf16[192,2048]{1,0:T(8,128)(2,1)}, bf16[192,2048]{1,0:T(8,128)(2,1)}, u32[]{:S(2)}, u32[]{:S(2)}) %collective-permute-start.1) | collective-permute-done | bytes 786464 | tf_op jit(solution)/shard_map/ppermute | solution.py:694
  47.6 270.3 %conditional.1 = (bf16[1024,2048]{1,0:T(8,128)(2,1)}) conditional(s32[]{:T(128)} %bitcast.2, (bf16[16,128]{1,0:T(8,128)(2,1)}, f32[2,16,128]{2,1,0:T(8,128)}, s32[8,128]{1,0:T(8,128)}, bf16[192,2048]{1,0:T(8,128)(2,1)}, bf16[192,2048]{1,0:T(8,128)(2,1)}, /*index=5*/bf16[192,2048]{1,0:T(8,128)(2,1)}, bf16[192,2048]{1,0:T(8,128)(2,1)}, ...), branch_computations={%region_0.0_spmd, %region_1.0_spmd, %region_2.0_spmd} | conditional | flops 137438953472 | bytes 268435456 | solution.py:699
  47.6 270.1 %mlp_block.3 = (bf16[1024,2048]{1,0:T(8,128)(2,1)}, bf16[2048,4096]{1,0:T(8,128)(2,1)}, bf16[4096,2048]{1,0:T(8,128)(2,1)}, f32[8,2048]{1,0:T(8,128)}) custom-call(bf16[16,128]{1,0:T(8,128)(2,1)} %get-tuple-element.74.gain_ref, f32[2,16,128]{2,1,0:T(8,128)} %get-tuple-element.76.place_ref, s32[8,128]{1,0:T(8,128)} %get-tuple-element.77.counts_ref, ...), custom_call_target="tpu_custom_call" | custom-call | flops 137438953472 | bytes 268435456 | tf_op jit(solution)/shard_map/cond/branch_0_fun/mlp_block/pallas_call | solution.py:621
  317.9 3.6 %copy_out.1 = bf16[1024,2048]{1,0:T(8,128)(2,1)} custom-call(bf16[1024,2048]{1,0:T(8,128)(2,1)} %get-tuple-element.127.src_ref), custom_call_target="tpu_custom_call" | custom-call | tf_op jit(solution)/shard_map/copy_out/pallas_call | solution.py:669
  (1 shorter events, 0.0 us)
Async XLA Ops:
  0.0 0.7 copy-start
  10.0 33.9 %collective-permute-start.2 = (bf16[192,2048]{1,0:T(8,128)(2,1)}, bf16[192,2048]{1,0:T(8,128)(2,1)}, u32[]{:S(2)}, u32[]{:S(2)}) collective-permute-start(bf16[192,2048]{1,0:T(8,128)(2,1)} %get-tuple-element.124), channel_id=1, source_target_pairs={{0,3},{1,2},{2,1},{3,0},{4,7},{5,6},{6,5},{7,4}} | collective-permute-start | bytes 2359304 | tf_op jit(solution)/shard_map/ppermute | solution.py:695
  12.7 35.0 %collective-permute-start.1 = (bf16[192,2048]{1,0:T(8,128)(2,1)}, bf16[192,2048]{1,0:T(8,128)(2,1)}, u32[]{:S(2)}, u32[]{:S(2)}) collective-permute-start(bf16[192,2048]{1,0:T(8,128)(2,1)} %get-tuple-element.125), channel_id=1, source_target_pairs={{0,2},{1,3},{2,0},{3,1},{4,6},{5,7},{6,4},{7,5}} | collective-permute-start | bytes 2359304 | tf_op jit(solution)/shard_map/ppermute | solution.py:694
  39.0 4.8 %collective-permute-start = (s32[1,128]{1,0:T(1,128)S(1)}, s32[1,128]{1,0:T(1,128)S(1)}, u32[]{:S(2)}, u32[]{:S(2)}) collective-permute-start(s32[1,128]{1,0:T(1,128)S(1)} %get-tuple-element.122), channel_id=1, source_target_pairs={{0,4},{4,0},{1,5},{5,1},{2,6},{6,2},{3,7},{7,3}} | collective-permute-start | bytes 1544 | tf_op jit(solution)/shard_map/ppermute | solution.py:698
